TPU v7x, 1024 devices: a whole 4x8x16 slice. The times are simulated.
1024 devices in a mesh: node: 32 (over z, core), dev: 32 (over y, x).
Axes of the slice: x: 4, y: 8, z: 16, core: 2. Of those that a mesh axis runs over, the one named last changes fastest.
Arguments:
- blocks: bfloat16 [32, 32, 16, 7, 16, 256], P('node', 'dev'), may hold values from -6 to 6
- levels: int32 [32, 32, 16], P('node', 'dev'), may hold values from 0 to 3
- destinations: int32 [32, 32, 16], P('node', 'dev'), may hold values from 0 to 31, as said below
- speeds: float32 [7], replicated, may hold values from -1 to 1
- thresholds: float32 [7], replicated, may hold values from 0.1 to 1
Outputs:
- updated: bfloat16 [32, 32, 32, 7, 16, 256], P('node', 'dev')
- new_levels: int32 [32, 32, 32], P('node', 'dev')
Inputs may be any that keep to these rules, and one draw needn't show every extreme that they name: `destinations`: at most 1 block of one device go to one device, and at most 32 blocks arrive at one device; in every group both bounds are reached.
All inputs are finite; a program needn't handle non-finite values.
Results may differ from a plain program's by a relative error of at most 0.001.
Values may be sent and summed in bfloat16 or wider, within the bound.
No kernel may reach another device: no remote copies, remote signals or barrier semaphores. Data moves between devices by JAX's collectives and lax.ppermute only.
A program may use at most 32 MiB of HBM per device.

v0:
```python
import jax
import jax.numpy as jnp
from jax import lax
from jax.sharding import PartitionSpec as P

QUANT = 7
EDGE = 16
SLOTS = 16
NEW_CAP = 32


COURANT = 0.4
WENO_EPS = 1e-06


def extended_2(block, sides, width):
    for axis, dim in sides:
        count = lax.axis_size(axis)
        forward = [(i, i + 1) for i in range(count - 1)]
        backward = [(target, source) for source, target in forward]
        low = lax.ppermute(
            lax.slice_in_dim(block, block.shape[dim] - width, None, axis=dim), axis, forward
        )
        high = lax.ppermute(lax.slice_in_dim(block, 0, width, axis=dim), axis, backward)
        block = jnp.concatenate([low, block, high], axis=dim)
    return block


def square(value):
    return value * value


def weno_face(first, second, third, fourth, fifth):
    guess_zero = (2.0 * first - 7.0 * second + 11.0 * third) / 6.0
    guess_one = (-second + 5.0 * third + 2.0 * fourth) / 6.0
    guess_two = (2.0 * third + 5.0 * fourth - fifth) / 6.0
    smooth_zero = 13.0 / 12.0 * square(first - 2.0 * second + third) + 0.25 * square(
        first - 4.0 * second + 3.0 * third
    )
    smooth_one = 13.0 / 12.0 * square(second - 2.0 * third + fourth) + 0.25 * square(
        second - fourth
    )
    smooth_two = 13.0 / 12.0 * square(third - 2.0 * fourth + fifth) + 0.25 * square(
        3.0 * third - 4.0 * fourth + fifth
    )
    weight_zero = 0.1 / square(WENO_EPS + smooth_zero)
    weight_one = 0.6 / square(WENO_EPS + smooth_one)
    weight_two = 0.3 / square(WENO_EPS + smooth_two)
    total = weight_zero + weight_one + weight_two
    return (weight_zero * guess_zero + weight_one * guess_one + weight_two * guess_two) / total


def shape_ghosts(near_layers, near_tag, own_tag):
    same_level = near_layers[:, :, 0:3]
    finer_level = 0.5 * (near_layers[:, :, 0:6:2] + near_layers[:, :, 1:6:2])
    coarser = jnp.concatenate(
        [near_layers[:, :, 0:1], near_layers[:, :, 0:1], near_layers[:, :, 1:2]], axis=2
    )
    offset = jnp.clip(near_tag - own_tag, -1, 1)[:, None, None, None]
    ghost_cells = jnp.where(offset > 0, finer_level, jnp.where(offset < 0, coarser, same_level))
    return lax.optimization_barrier(ghost_cells.astype(jnp.bfloat16))


def advance_quantity(extended, occupied, velocity, threshold):
    cells = extended.shape[1] - 6
    stencil = [extended[:, k : k + cells + 1] for k in range(6)]
    left_state = weno_face(stencil[0], stencil[1], stencil[2], stencil[3], stencil[4])
    right_state = weno_face(stencil[5], stencil[4], stencil[3], stencil[2], stencil[1])
    fluxes = jnp.maximum(velocity, 0.0) * left_state + jnp.minimum(velocity, 0.0) * right_state
    advanced = extended[:, 3 : 3 + cells] - COURANT * (fluxes[:, 1:] - fluxes[:, :-1])
    even_cells = advanced[:, 0::2]
    odd_cells = advanced[:, 1::2]
    predicted = jnp.concatenate(
        [0.5 * (even_cells[:, :-1] + even_cells[:, 1:]), even_cells[:, -1:]], axis=1
    )
    detail = odd_cells - predicted
    kept_cells = predicted + detail - jnp.clip(detail, -threshold, threshold)
    result = jnp.stack([even_cells, kept_cells], axis=2).reshape(advanced.shape)
    return jnp.where(occupied[:, None, None], result, 0.0).astype(jnp.bfloat16)


def body(blocks, levels, destinations, speeds, thresholds):
    owners = lax.axis_size("dev")
    pair_slots = max(1, (2 * SLOTS + owners - 1) // owners)
    send_rows = owners * pair_slots
    plane_cells = EDGE * EDGE
    targets = destinations[0, 0]
    matches = (targets[:, None] == jnp.arange(owners, dtype=jnp.int32)[None, :]).astype(jnp.int32)
    within = jnp.sum((jnp.cumsum(matches, axis=0) - matches) * matches, axis=1)
    buffer_row = targets * pair_slots + within
    placing = (buffer_row[None, :] == jnp.arange(send_rows, dtype=jnp.int32)[:, None]).astype(
        jnp.bfloat16
    )
    payload = blocks.reshape(SLOTS, QUANT * EDGE * plane_cells)
    outgoing = jnp.dot(placing, payload, preferred_element_type=jnp.float32).astype(jnp.bfloat16)
    level_tags = (levels[0, 0] + 1).astype(jnp.bfloat16)[:, None]
    outgoing_tags = jnp.dot(placing, level_tags, preferred_element_type=jnp.float32).astype(
        jnp.bfloat16
    )[:, 0]
    incoming, incoming_tags = (
        lax.all_to_all(outgoing, "dev", split_axis=0, concat_axis=0, tiled=True),
        lax.all_to_all(outgoing_tags, "dev", split_axis=0, concat_axis=0, tiled=True),
    )
    present = (incoming_tags > 0).astype(jnp.int32)
    packed_rank = jnp.cumsum(present) - present
    packing = (
        (packed_rank[None, :] == jnp.arange(NEW_CAP, dtype=jnp.int32)[:, None])
        & (present[None, :] > 0)
    ).astype(jnp.bfloat16)
    arranged = jnp.dot(packing, incoming, preferred_element_type=jnp.float32).astype(jnp.bfloat16)
    arranged = arranged.reshape(NEW_CAP, QUANT, EDGE, plane_cells)
    block_tag = jnp.dot(packing, incoming_tags[:, None], preferred_element_type=jnp.float32)[
        :, 0
    ].astype(jnp.int32)
    near_tags = extended_2(block_tag[:, None], (("node", 1),), 1)
    top_layers = arranged[:, :, EDGE - 6 :].astype(jnp.float32)[:, :, ::-1]
    bottom_layers = arranged[:, :, :6].astype(jnp.float32)
    for_above = shape_ghosts(top_layers, block_tag, near_tags[:, 2])[:, :, ::-1]
    for_below = shape_ghosts(bottom_layers, block_tag, near_tags[:, 0])
    received = extended_2(jnp.concatenate([for_below, for_above], axis=2), (("node", 2),), 3)
    ghost_low = received[:, :, 0:3]
    ghost_high = received[:, :, 9:12]
    extended = jnp.concatenate([ghost_low, arranged, ghost_high], axis=2).astype(jnp.float32)
    extended = jnp.moveaxis(extended, 1, 0)
    occupied = block_tag > 0
    result = lax.map(
        lambda entry: advance_quantity(entry[0], occupied, entry[1], entry[2]),
        (extended, speeds, thresholds),
    )
    updated = jnp.moveaxis(result, 0, 1).reshape(1, 1, NEW_CAP, QUANT, EDGE, plane_cells)
    new_levels = (block_tag - 1).reshape(1, 1, NEW_CAP)
    return (updated, new_levels)


def solution(mesh):
    return jax.shard_map(
        body,
        mesh=mesh,
        in_specs=(
            P("node", "dev", None, None, None, None),
            P("node", "dev", None),
            P("node", "dev", None),
            P(),
            P(),
        ),
        out_specs=(P("node", "dev", None, None, None, None), P("node", "dev", None)),
        check_vma=False,
    )
```

profile of v0, /device:TPU:195, one launch (start us, length us, event | category | flops | bytes accessed | tf_op | source)
XLA Modules:
  0.0 175.2 jit_solution(12497463913313676774)
XLA Ops:
  0.6 0.7 fusion.44
  1.4 0.8 select_reduce_fusion
  2.2 0.7 bitcast_add_fusion
  2.9 0.8 fusion.31
  3.7 0.7 copy.43
  4.4 9.7 %all-to-all-start = ((bf16[32,1,1]{2,1,0:T(2,128)(2,1)}), bf16[32,1,1]{2,1,0:T(2,128)(2,1)S(1)}, u32[]{:S(2)}, u32[]{:S(2)}) async-start(bf16[32,1,1]{2,1,0:T(2,128)(2,1)} %copy.43), calls=%async_computation | async-start | bytes 32768 | tf_op jit(solution)/shard_map/all_to_all | solution.py:102
  14.1 1.6 reshape.146
  15.7 1.9 %fusion.27 = bf16[32,1,28672]{2,0,1:T(8,128)(2,1)} fusion(bf16[16,28672]{1,0:T(8,128)(2,1)S(1)} %reshape.146, s32[16]{0:T(128)S(1)} %bitcast_add_fusion), kind=kOutput, calls=%fused_computation.43 | convolution fusion | flops 30278144 | bytes 2752576 | tf_op jit(solution)/shard_map/dot_general | solution.py:95
  18.1 3.6 %reduce.3 = bf16[32,28672]{1,0:T(8,128)(2,1)S(1)} reduce(bf16[32,1,28672]{2,0,1:T(8,128)(2,1)} %fusion.27, bf16[]{:T(256)} %broadcast.162), dimensions={1}, to_apply=%copy.45.reduce_sub_computation | reduce | bytes 3670018 | tf_op jit(solution)/shard_map/all_to_all | solution.py:101
  21.6 2.3 %reshape.158 = bf16[32,2,14336]{2,1,0:T(2,128)(2,1)} reshape(bf16[32,28672]{1,0:T(8,128)(2,1)S(1)} %reduce.3) | data formatting | bytes 3670016
  23.9 9.2 %all-to-all-start.1 = ((bf16[32,2,14336]{2,1,0:T(2,128)(2,1)}), bf16[32,2,14336]{2,1,0:T(2,128)(2,1)S(1)}, u32[]{:S(2)}, u32[]{:S(2)}) async-start(bf16[32,2,14336]{2,1,0:T(2,128)(2,1)} %reshape.158), calls=%async_computation.1 | async-start | bytes 3670016 | tf_op jit(solution)/shard_map/all_to_all | solution.py:101
  33.8 3.7 %collective-permute-start = (s32[32,1]{0,1:T(1,128)S(1)}, s32[32,1]{0,1:T(1,128)S(1)}, u32[]{:S(2)}, u32[]{:S(2)}) collective-permute-start(s32[32,1]{0,1:T(1,128)S(1)} %bitcast.88), channel_id=1, source_target_pairs={{32,0},{64,32},{96,64},{128,96},{160,128},{192,160},{224,192},{256... | collective-permute-start | bytes 392 | tf_op jit(solution)/shard_map/ppermute | solution.py:24
  37.5 5.1 %collective-permute-start.2 = (s32[32,1]{0,1:T(1,128)S(1)}, s32[32,1]{0,1:T(1,128)S(1)}, u32[]{:S(2)}, u32[]{:S(2)}) collective-permute-start(s32[32,1]{0,1:T(1,128)S(1)} %bitcast.89), channel_id=1, source_target_pairs={{0,32},{32,64},{64,96},{96,128},{128,160},{160,192},{192,224},{224... | collective-permute-start | bytes 392 | tf_op jit(solution)/shard_map/ppermute | solution.py:21
  42.7 0.7 collective-permute-done.2
  44.0 31.5 %all-to-all-done.1 = bf16[32,2,14336]{2,1,0:T(2,128)(2,1)S(1)} async-done(((bf16[32,2,14336]{2,1,0:T(2,128)(2,1)}), bf16[32,2,14336]{2,1,0:T(2,128)(2,1)S(1)}, u32[]{:S(2)}, u32[]{:S(2)}) %all-to-all-start.1) | async-done | bytes 1835040 | tf_op jit(solution)/shard_map/all_to_all | solution.py:101
  75.5 6.5 %reshape.159 = bf16[32,1,28672]{2,1,0:T(2,128)(2,1)} reshape(bf16[32,2,14336]{2,1,0:T(2,128)(2,1)S(1)} %all-to-all-done.1) | data formatting | bytes 3670016
  82.0 4.5 %convolution_convert_fusion.1 = bf16[32,28672]{1,0:T(8,128)(2,1)S(1)} fusion(bf16[32,1,28672]{2,1,0:T(2,128)(2,1)} %reshape.159, s32[32]{0:T(128)S(1)} %fusion.52, pred[32]{0:T(512)(128)(4,1)S(1)} %fusion.51), kind=kOutput, calls=%fused_computation.42 | convolution fusion | flops 59639808 | bytes 3670176 | tf_op jit(solution)/shard_map/dot_general | solution.py:110
  86.9 0.7 copy.46
  88.0 0.7 slice.125
  88.7 0.7 slice.124
  89.8 0.7 rev.4
  90.5 8.9 %collective-permute-start.1 = (bf16[32,7,3,256]{3,0,2,1:T(8,128)(2,1)}, bf16[32,7,3,256]{3,0,2,1:T(8,128)(2,1)}, u32[]{:S(2)}, u32[]{:S(2)}) collective-permute-start(bf16[32,7,3,256]{3,0,2,1:T(8,128)(2,1)} %rev.4), channel_id=1, source_target_pairs={{0,32},{32,64},{64,96},{96,128},{128,160},{160,192},{192,224},{224... | collective-permute-start | bytes 1032200 | tf_op jit(solution)/shard_map/ppermute | solution.py:21
  99.5 1.3 fusion.34
  100.8 1.9 %collective-permute-start.3 = (bf16[32,7,3,256]{3,0,2,1:T(8,128)(2,1)S(1)}, bf16[32,7,3,256]{3,0,2,1:T(8,128)(2,1)S(1)}, u32[]{:S(2)}, u32[]{:S(2)}) collective-permute-start(bf16[32,7,3,256]{3,0,2,1:T(8,128)(2,1)S(1)} %fusion.34), channel_id=1, source_target_pairs={{32,0},{64,32},{96,64},{128,96},{160,128},{192,160},{224,192},{256... | collective-permute-start | bytes 1032200 | tf_op jit(solution)/shard_map/ppermute | solution.py:24
  102.8 1.1 add_bitcast_fusion
  104.0 6.6 %collective-permute-done.3 = bf16[32,7,3,256]{3,0,2,1:T(8,128)(2,1)S(1)} collective-permute-done((bf16[32,7,3,256]{3,0,2,1:T(8,128)(2,1)S(1)}, bf16[32,7,3,256]{3,0,2,1:T(8,128)(2,1)S(1)}, u32[]{:S(2)}, u32[]{:S(2)}) %collective-permute-start.3) | collective-permute-done | bytes 344096 | tf_op jit(solution)/shard_map/ppermute | solution.py:24
  110.6 3.6 %convert_bitcast_fusion = f32[7,32,22,256]{3,1,2,0:T(8,128)} fusion(bf16[32,7,3,256]{3,0,2,1:T(8,128)(2,1)S(1)} %collective-permute-done.3, bf16[32,7,16,256]{3,0,2,1:T(8,128)(2,1)S(1)} %copy.46, bf16[32,7,3,256]{3,0,2,1:T(8,128)(2,1)} %collective-permute-done.1), kind=kLoop, calls=%fused_computation.44 | loop fusion | flops 3784704 | bytes 7569408 | tf_op jit(solution)/shard_map/transpose | solution.py:124
  114.2 61.0 %while.10 = (s32[]{:T(128)}, bf16[7,32,16,256]{3,2,0,1:T(8,128)(2,1)}, pred[32]{0:T(512)(128)(4,1)S(1)}, f32[7,32,22,256]{3,1,2,0:T(8,128)}, f32[7]{0:T(128)S(1)}, /*index=5*/f32[7]{0:T(128)S(1)}, s32[]{:T(128)}, f32[1]{0:T(128)}) while((s32[]{:T(128)}, bf16[7,32,16,256]{3,2,0,1:T(8,128)(2,1)}, pred[32]{0:T(512)(128)(4,1)S(1)}, ...), condition=%wide.region_4.5_spmd, body=%wide.region_3.4_spmd.sunk | while | flops 18915332 | bytes 11731649 | solution.py:126
  114.2 0.6 dynamic_slice.16
  116.1 1.2 dynamic-slice_bitcast_fusion.2
  117.3 2.5 %multiply_add_fusion.4 = f32[32,17,256]{2,0,1:T(8,128)S(1)} fusion(f32[32,22,256]{2,0,1:T(8,128)S(1)} %dynamic-slice_bitcast_fusion.2, f32[]{:T(128)} %bitcast.80, f32[]{:T(128)} %bitcast.81), kind=kLoop, calls=%fused_computation.1.clone.1 | loop fusion | flops 17686528 | bytes 3899400 | tf_op jit(solution)/shard_map/while/body/eval_jaxpr/add | solution.py:69
  119.9 0.6 dynamic_slice.17
  121.2 0.7 slice_bitcast_fusion.2
  122.1 0.9 copy_dynamic-update-slice_fusion.2
  124.8 1.2 dynamic-slice_bitcast_fusion.2
  126.0 2.5 %multiply_add_fusion.4 = f32[32,17,256]{2,0,1:T(8,128)S(1)} fusion(f32[32,22,256]{2,0,1:T(8,128)S(1)} %dynamic-slice_bitcast_fusion.2, f32[]{:T(128)} %bitcast.80, f32[]{:T(128)} %bitcast.81), kind=kLoop, calls=%fused_computation.1.clone.1 | loop fusion | flops 17686528 | bytes 3899400 | tf_op jit(solution)/shard_map/while/body/eval_jaxpr/add | solution.py:69
  128.6 0.6 dynamic_slice.17
  129.9 0.7 slice_bitcast_fusion.2
  130.8 0.9 copy_dynamic-update-slice_fusion.2
  133.5 1.2 dynamic-slice_bitcast_fusion.2
  134.7 2.5 %multiply_add_fusion.4 = f32[32,17,256]{2,0,1:T(8,128)S(1)} fusion(f32[32,22,256]{2,0,1:T(8,128)S(1)} %dynamic-slice_bitcast_fusion.2, f32[]{:T(128)} %bitcast.80, f32[]{:T(128)} %bitcast.81), kind=kLoop, calls=%fused_computation.1.clone.1 | loop fusion | flops 17686528 | bytes 3899400 | tf_op jit(solution)/shard_map/while/body/eval_jaxpr/add | solution.py:69
  137.4 0.6 dynamic_slice.17
  138.6 0.7 slice_bitcast_fusion.2
  139.5 0.9 copy_dynamic-update-slice_fusion.2
  142.2 1.2 dynamic-slice_bitcast_fusion.2
  143.4 2.5 %multiply_add_fusion.4 = f32[32,17,256]{2,0,1:T(8,128)S(1)} fusion(f32[32,22,256]{2,0,1:T(8,128)S(1)} %dynamic-slice_bitcast_fusion.2, f32[]{:T(128)} %bitcast.80, f32[]{:T(128)} %bitcast.81), kind=kLoop, calls=%fused_computation.1.clone.1 | loop fusion | flops 17686528 | bytes 3899400 | tf_op jit(solution)/shard_map/while/body/eval_jaxpr/add | solution.py:69
  146.1 0.6 dynamic_slice.17
  147.3 0.7 slice_bitcast_fusion.2
  148.2 0.9 copy_dynamic-update-slice_fusion.2
  150.9 1.2 dynamic-slice_bitcast_fusion.2
  152.1 2.5 %multiply_add_fusion.4 = f32[32,17,256]{2,0,1:T(8,128)S(1)} fusion(f32[32,22,256]{2,0,1:T(8,128)S(1)} %dynamic-slice_bitcast_fusion.2, f32[]{:T(128)} %bitcast.80, f32[]{:T(128)} %bitcast.81), kind=kLoop, calls=%fused_computation.1.clone.1 | loop fusion | flops 17686528 | bytes 3899400 | tf_op jit(solution)/shard_map/while/body/eval_jaxpr/add | solution.py:69
  154.8 0.6 dynamic_slice.17
  156.0 0.7 slice_bitcast_fusion.2
  156.9 0.9 copy_dynamic-update-slice_fusion.2
  159.7 1.2 dynamic-slice_bitcast_fusion.2
  160.8 2.5 %multiply_add_fusion.4 = f32[32,17,256]{2,0,1:T(8,128)S(1)} fusion(f32[32,22,256]{2,0,1:T(8,128)S(1)} %dynamic-slice_bitcast_fusion.2, f32[]{:T(128)} %bitcast.80, f32[]{:T(128)} %bitcast.81), kind=kLoop, calls=%fused_computation.1.clone.1 | loop fusion | flops 17686528 | bytes 3899400 | tf_op jit(solution)/shard_map/while/body/eval_jaxpr/add | solution.py:69
  163.5 0.6 dynamic_slice.17
  164.7 0.7 slice_bitcast_fusion.2
  165.6 0.9 copy_dynamic-update-slice_fusion.2
  168.4 1.2 dynamic-slice_bitcast_fusion.2
  169.6 2.5 %multiply_add_fusion.4 = f32[32,17,256]{2,0,1:T(8,128)S(1)} fusion(f32[32,22,256]{2,0,1:T(8,128)S(1)} %dynamic-slice_bitcast_fusion.2, f32[]{:T(128)} %bitcast.80, f32[]{:T(128)} %bitcast.81), kind=kLoop, calls=%fused_computation.1.clone.1 | loop fusion | flops 17686528 | bytes 3899400 | tf_op jit(solution)/shard_map/while/body/eval_jaxpr/add | solution.py:69
  172.2 0.6 dynamic_slice.17
  173.5 0.7 slice_bitcast_fusion.2
  174.3 0.9 copy_dynamic-update-slice_fusion.2
  (87 shorter events, 8.8 us)
Async XLA Ops:
  4.4 19.5 %all-to-all-start = ((bf16[32,1,1]{2,1,0:T(2,128)(2,1)}), bf16[32,1,1]{2,1,0:T(2,128)(2,1)S(1)}, u32[]{:S(2)}, u32[]{:S(2)}) async-start(bf16[32,1,1]{2,1,0:T(2,128)(2,1)} %copy.43), calls=%async_computation | async-start | bytes 32768 | tf_op jit(solution)/shard_map/all_to_all | solution.py:102
  23.9 51.6 %all-to-all-start.1 = ((bf16[32,2,14336]{2,1,0:T(2,128)(2,1)}), bf16[32,2,14336]{2,1,0:T(2,128)(2,1)S(1)}, u32[]{:S(2)}, u32[]{:S(2)}) async-start(bf16[32,2,14336]{2,1,0:T(2,128)(2,1)} %reshape.158), calls=%async_computation.1 | async-start | bytes 3670016 | tf_op jit(solution)/shard_map/all_to_all | solution.py:101
  33.8 48.2 %copy-start.3 = (s32[32]{0:T(128)}, s32[32]{0:T(128)S(1)}, u32[]{:S(2)}) copy-start(s32[32]{0:T(128)S(1)} %fusion.32) | copy-start | bytes 388
  33.8 8.8 %collective-permute-start = (s32[32,1]{0,1:T(1,128)S(1)}, s32[32,1]{0,1:T(1,128)S(1)}, u32[]{:S(2)}, u32[]{:S(2)}) collective-permute-start(s32[32,1]{0,1:T(1,128)S(1)} %bitcast.88), channel_id=1, source_target_pairs={{32,0},{64,32},{96,64},{128,96},{160,128},{192,160},{224,192},{256... | collective-permute-start | bytes 392 | tf_op jit(solution)/shard_map/ppermute | solution.py:24
  37.5 5.8 %collective-permute-start.2 = (s32[32,1]{0,1:T(1,128)S(1)}, s32[32,1]{0,1:T(1,128)S(1)}, u32[]{:S(2)}, u32[]{:S(2)}) collective-permute-start(s32[32,1]{0,1:T(1,128)S(1)} %bitcast.89), channel_id=1, source_target_pairs={{0,32},{32,64},{64,96},{96,128},{128,160},{160,192},{192,224},{224... | collective-permute-start | bytes 392 | tf_op jit(solution)/shard_map/ppermute | solution.py:21
  87.8 1.6 copy-start.1
  87.8 1.6 copy-start.2
  90.5 13.4 %collective-permute-start.1 = (bf16[32,7,3,256]{3,0,2,1:T(8,128)(2,1)}, bf16[32,7,3,256]{3,0,2,1:T(8,128)(2,1)}, u32[]{:S(2)}, u32[]{:S(2)}) collective-permute-start(bf16[32,7,3,256]{3,0,2,1:T(8,128)(2,1)} %rev.4), channel_id=1, source_target_pairs={{0,32},{32,64},{64,96},{96,128},{128,160},{160,192},{192,224},{224... | collective-permute-start | bytes 1032200 | tf_op jit(solution)/shard_map/ppermute | solution.py:21
  100.8 9.8 %collective-permute-start.3 = (bf16[32,7,3,256]{3,0,2,1:T(8,128)(2,1)S(1)}, bf16[32,7,3,256]{3,0,2,1:T(8,128)(2,1)S(1)}, u32[]{:S(2)}, u32[]{:S(2)}) collective-permute-start(bf16[32,7,3,256]{3,0,2,1:T(8,128)(2,1)S(1)} %fusion.34), channel_id=1, source_target_pairs={{32,0},{64,32},{96,64},{128,96},{160,128},{192,160},{224,192},{256... | collective-permute-start | bytes 1032200 | tf_op jit(solution)/shard_map/ppermute | solution.py:24
  103.9 10.3 %copy-start = (pred[32]{0:T(512)(128)(4,1)S(1)}, pred[32]{0:T(512)(128)(4,1)}, u32[]{:S(2)}) copy-start(pred[32]{0:T(512)(128)(4,1)} %get-tuple-element.105) | copy-start | bytes 100
  103.9 10.3 %copy-start.4 = (f32[7]{0:T(128)S(1)}, f32[7]{0:T(128)}, u32[]{:S(2)}) copy-start(f32[7]{0:T(128)} %param.10) | copy-start | bytes 88
  103.9 10.3 %copy-start.5 = (f32[7]{0:T(128)S(1)}, f32[7]{0:T(128)}, u32[]{:S(2)}) copy-start(f32[7]{0:T(128)} %param.11) | copy-start | bytes 88
where the time goes:
time: 176 us; the launch traced here: 175 us
  waiting for transfers between devices  38.9 us (22%)
  starting transfers between devices  38.5 us (22%)
  local copies, waits for them, and re-layouts  38.1 us (22%)
  other arithmetic  37.7 us (21%)
  loops' own time  13.9 us (8%)
  matrix products  7.26 us (4%)
    all_to_all x1, waiting for transfers between devices, body(): lax.all_to_all(outgoing, 'dev', split_axis=0, concat_axis=0, tiled=True)  31.5 us
    add x7, other arithmetic, advance_quantity(): jnp.maximum(velocity, 0.0) * left_state  17.4 us
    ppermute x2, starting transfers between devices, extended_2(): lax.ppermute(lax.slice_in_dim(block, block.shape[dim] - width, None, axis...  14 us
    another operation x1, loops' own time, body(): lax.map(lambda entry: advance_quantity(entry[0], occupied, entry[1], entr...  13.9 us
    all_to_all x1, starting transfers between devices, body(): lax.all_to_all(outgoing_tags, 'dev', split_axis=0, concat_axis=0, tiled=T...  9.69 us
    all_to_all x1, starting transfers between devices, body(): lax.all_to_all(outgoing, 'dev', split_axis=0, concat_axis=0, tiled=True)  9.22 us
    unnamed x15, local copies, waits for them, and re-layouts  9.19 us
    dynamic_slice x14, local copies, waits for them, and re-layouts, body(): lax.map(lambda entry: advance_quantity(entry[0], occupied, entry[1], entr...  8.53 us
  transfers between devices with their start and end apart: 6, of which 4 were waited for; matrix products, arithmetic and copies ran while one was open for 8% of the time, Pallas kernels for 0%

commit v1 on v0

v1 whole, which is shorter than its diff:
```python
import jax
import jax.numpy as jnp
from jax import lax
from jax.experimental import pallas as pl
from jax.experimental.pallas import tpu as pltpu
from jax.sharding import PartitionSpec as P

QUANT = 7
EDGE = 16
PLANE = EDGE * EDGE
SLOTS = 16
NEW_CAP = 32
LANES = 128
HALVES = PLANE // LANES
PITCH = EDGE + 1

COURANT = 0.4
WENO_EPS = 1e-06

SMEM = pl.BlockSpec(memory_space=pltpu.SMEM)
VMEM = pl.BlockSpec(memory_space=pltpu.VMEM)
ANY = pl.BlockSpec(memory_space=pl.ANY)


def label_kernel(dest_ref, level_ref, out_ref):
    row = lax.broadcasted_iota(jnp.int32, out_ref.shape, 0)
    tags = jnp.zeros(out_ref.shape, jnp.int32)
    for s in range(SLOTS):
        tags = jnp.where(row == dest_ref[0, 0, s], level_ref[0, 0, s] + 1, tags)
    out_ref[...] = tags


def pack_kernel(dest_ref, blocks_ref, out_ref, sems):
    copies = [
        pltpu.make_async_copy(blocks_ref.at[s], out_ref.at[dest_ref[0, 0, s]], sems.at[s])
        for s in range(SLOTS)
    ]
    for copy in copies:
        copy.start()
    for copy in copies:
        copy.wait()


def rank_kernel(tags_sm, tags_ref, source_ref, count_ref, new_ref, own_ref):
    own_ref[...] = jnp.zeros_like(own_ref)
    for p in range(NEW_CAP):
        source_ref[p] = 0
        new_ref[p] = -1
    count = jnp.int32(0)
    for i in range(NEW_CAP):
        tag = tags_sm[i, 0]
        here = tag > 0

        @pl.when(here)
        def _(i=i, tag=tag, count=count):
            source_ref[count] = i
            new_ref[count] = tag - 1
            own_ref[pl.ds(count, 1), :] = tags_ref[pl.ds(i, 1), :]

        count = count + here.astype(jnp.int32)
    count_ref[0] = count


def shaped(layers, finer, coarser):
    result = []
    for m in (1, 2, 3):
        same = layers[m - 1]
        fine = 0.5 * (layers[2 * m - 2] + layers[2 * m - 1])
        coarse = layers[(m + 1) // 2 - 1]
        result.append(jnp.where(finer, fine, jnp.where(coarser, coarse, same)))
    return result


def arrange_kernel(
    source_ref, count_ref, own_ref, low_ref, high_ref, in_ref, out_ref, below_ref, above_ref, work
):
    count = count_ref[0]
    own = own_ref[...]
    low = low_ref[...]
    high = high_ref[...]
    for half in range(HALVES):
        lanes = slice(half * LANES, (half + 1) * LANES)
        for p in range(NEW_CAP):
            cells = in_ref[source_ref[p], 0, :, lanes].astype(jnp.float32)
            work[half, p * PITCH : p * PITCH + EDGE, :] = jnp.where(p < count, cells, 0.0)
        layers = []
        for c in range(EDGE):
            layer = work[half, pl.ds(c, NEW_CAP, stride=PITCH), :]
            out_ref[0, c, :, lanes] = layer.astype(jnp.bfloat16)
            layers.append(layer)
            if c == 5:
                for m, ghost in enumerate(shaped(layers, own > low, own < low)):
                    below_ref[0, m, :, lanes] = ghost.astype(jnp.bfloat16)
        top = layers[: EDGE - 7 : -1]
        for m, ghost in enumerate(shaped(top, own > high, own < high)):
            above_ref[0, m, :, lanes] = ghost.astype(jnp.bfloat16)


def face_ratios(read):
    cells, steps, halves, wides, curves = [], [], [], [], []
    for k in range(EDGE + 6):
        cells.append(read(k))
        if k >= 1:
            step = cells[k] - cells[k - 1]
            half = 0.5 * step
            steps.append(step)
            halves.append(half)
            wides.append(step + half)
        if k >= 2:
            bend = steps[k - 1] - steps[k - 2]
            curves.append((13.0 / 12.0) * (bend * bend) + WENO_EPS)
        if k >= 4:
            f = k - 4
            one = wides[f + 1] - halves[f]
            two = halves[f + 1] + halves[f + 2]
            three = wides[f + 2] - halves[f + 3]
            p_zero = curves[f] + one * one
            p_one = curves[f + 1] + two * two
            p_two = curves[f + 2] + three * three
            w_zero = p_one * p_two
            w_one = p_zero * p_two
            w_two = p_zero * p_one
            w_zero = w_zero * w_zero
            w_one = 6.0 * (w_one * w_one)
            w_two = 3.0 * (w_two * w_two)
            g_zero = 2.5 * steps[f + 1] - steps[f]
            g_one = halves[f + 1] + steps[f + 2]
            g_two = 2.0 * steps[f + 2] - halves[f + 3]
            total = w_zero + w_one + w_two
            ratio = (w_zero * g_zero + w_one * g_one + w_two * g_two) / total
            yield cells[f + 2], ratio


def advance_kernel(
    speed_ref, limit_ref, count_ref, in_ref, low_ref, high_ref, out_ref, work
):
    count = count_ref[0]
    q = pl.program_id(0)
    speed = speed_ref[q]
    limit = limit_ref[q]
    rate = COURANT * jnp.abs(speed)
    third = rate / 3.0
    group = 16

    def run(forward):
        def tile(index, carry):
            half = index % HALVES
            base = pl.multiple_of((index // HALVES) * group, group)
            lanes = pl.ds(pl.multiple_of(half * LANES, LANES), LANES)
            rows = pl.ds(base, group)

            def read(k):
                k = k if forward else EDGE + 5 - k
                if k < 3:
                    part = low_ref[0, 2 - k, rows, lanes]
                elif k < EDGE + 3:
                    part = in_ref[0, k - 3, rows, lanes]
                else:
                    part = high_ref[0, k - EDGE - 3, rows, lanes]
                return part.astype(jnp.float32)

            advanced = {}

            def emit(c):
                slot = work.at[pl.ds(c, group, stride=PITCH), :]
                if c % 2 == 0:
                    slot[...] = advanced[c]
                    return
                if c == EDGE - 1:
                    guess = advanced[c - 1]
                else:
                    guess = 0.5 * (advanced[c - 1] + advanced[c + 1])
                detail = advanced[c] - guess
                slot[...] = guess + detail - jnp.clip(detail, -limit, limit)

            last = None
            for f, (centre, ratio) in enumerate(face_ratios(read)):
                flux = rate * centre + third * ratio
                if f >= 1:
                    k = f - 1
                    c = k if forward else EDGE - 1 - k
                    advanced[c] = read(k + 3) - (flux - last)
                    if c % 2 == 0:
                        emit(c)
                        if forward and c >= 2:
                            emit(c - 1)
                        if not forward:
                            emit(c + 1)
                last = flux
            if forward:
                emit(EDGE - 1)
            for p in range(group):
                cells = work[p * PITCH : p * PITCH + EDGE, :]
                cells = jnp.where(base + p < count, cells, 0.0)
                out_ref[base + p, 0, :, lanes] = cells.astype(jnp.bfloat16)
            return carry

        lax.fori_loop(0, HALVES * (NEW_CAP // group), tile, 0)

    @pl.when(speed >= 0.0)
    def _():
        run(True)

    @pl.when(speed < 0.0)
    def _():
        run(False)


def struct(shape, dtype):
    return jax.ShapeDtypeStruct(shape, dtype)


def body(blocks, levels, destinations, speeds, thresholds):
    owners = lax.axis_size("dev")
    count = lax.axis_size("node")
    up = [(i, i + 1) for i in range(count - 1)]
    down = [(i + 1, i) for i in range(count - 1)]
    labels = pl.pallas_call(
        label_kernel,
        in_specs=[SMEM, SMEM],
        out_specs=VMEM,
        out_shape=struct((owners, LANES), jnp.int32),
        name="label",
    )(destinations, levels)
    labels = lax.all_to_all(
        labels.reshape(owners, 1, LANES), "dev", split_axis=0, concat_axis=0, tiled=True
    ).reshape(owners, LANES)
    outgoing = pl.pallas_call(
        pack_kernel,
        in_specs=[SMEM, VMEM],
        out_specs=ANY,
        out_shape=struct((owners, QUANT, EDGE, PLANE), jnp.bfloat16),
        scratch_shapes=[pltpu.SemaphoreType.DMA((SLOTS,))],
        name="pack",
    )(destinations, blocks.reshape(SLOTS, QUANT, EDGE, PLANE))
    incoming = lax.all_to_all(outgoing, "dev", split_axis=0, concat_axis=0, tiled=True)
    source, total, new_levels, own = pl.pallas_call(
        rank_kernel,
        in_specs=[SMEM, VMEM],
        out_specs=(SMEM, SMEM, SMEM, VMEM),
        out_shape=(
            struct((NEW_CAP,), jnp.int32),
            struct((1,), jnp.int32),
            struct((NEW_CAP,), jnp.int32),
            struct((NEW_CAP, LANES), jnp.int32),
        ),
        name="rank",
    )(labels, labels)
    low_tag = lax.ppermute(own, "node", up)
    high_tag = lax.ppermute(own, "node", down)
    plane = (1, EDGE, NEW_CAP, PLANE)
    ghost = (1, 3, NEW_CAP, PLANE)
    natural = (NEW_CAP, 1, EDGE, PLANE)
    by_quantity = lambda q: (q, 0, 0, 0)
    arranged, for_below, for_above = pl.pallas_call(
        arrange_kernel,
        grid=(QUANT,),
        in_specs=[
            SMEM,
            SMEM,
            VMEM,
            VMEM,
            VMEM,
            pl.BlockSpec(natural, lambda q: (0, q, 0, 0)),
        ],
        out_specs=(
            pl.BlockSpec(plane, by_quantity),
            pl.BlockSpec(ghost, by_quantity),
            pl.BlockSpec(ghost, by_quantity),
        ),
        out_shape=(
            struct((QUANT, EDGE, NEW_CAP, PLANE), jnp.bfloat16),
            struct((QUANT, 3, NEW_CAP, PLANE), jnp.bfloat16),
            struct((QUANT, 3, NEW_CAP, PLANE), jnp.bfloat16),
        ),
        scratch_shapes=[pltpu.VMEM((HALVES, NEW_CAP * PITCH + 8, LANES), jnp.float32)],
        name="arrange",
    )(source, total, own, low_tag, high_tag, incoming)
    ghost_high = lax.ppermute(for_below, "node", down)
    ghost_low = lax.ppermute(for_above, "node", up)
    updated = pl.pallas_call(
        advance_kernel,
        grid=(QUANT,),
        in_specs=[
            SMEM,
            SMEM,
            SMEM,
            pl.BlockSpec(plane, by_quantity),
            pl.BlockSpec(ghost, by_quantity),
            pl.BlockSpec(ghost, by_quantity),
        ],
        out_specs=pl.BlockSpec(natural, lambda q: (0, q, 0, 0)),
        out_shape=struct((NEW_CAP, QUANT, EDGE, PLANE), jnp.bfloat16),
        scratch_shapes=[pltpu.VMEM((16 * PITCH + 8, LANES), jnp.float32)],
        name="advance",
    )(speeds, thresholds, total, arranged, ghost_low, ghost_high)
    return (
        updated.reshape(1, 1, NEW_CAP, QUANT, EDGE, PLANE),
        new_levels.reshape(1, 1, NEW_CAP),
    )


def solution(mesh):
    return jax.shard_map(
        body,
        mesh=mesh,
        in_specs=(
            P("node", "dev", None, None, None, None),
            P("node", "dev", None),
            P("node", "dev", None),
            P(),
            P(),
        ),
        out_specs=(P("node", "dev", None, None, None, None), P("node", "dev", None)),
        check_vma=False,
    )
```

time: 176 us -> 105 us (0.60)
  the two profiles are of different devices: /device:TPU:195 before, /device:TPU:449 now
where the time goes in v1:
time: 105 us; the launch traced here: 104 us
  waiting for transfers between devices  44.9 us (43%)
  starting transfers between devices  34.5 us (33%)
  Pallas kernels  21.5 us (20%)
  local copies, waits for them, and re-layouts  2.59 us (2%)
    all_to_all x1, waiting for transfers between devices, body(): lax.all_to_all(outgoing, 'dev', split_axis=0, concat_axis=0, tiled=True)  29.4 us
    ppermute x1, starting transfers between devices, body(): ghost_low = lax.ppermute(for_above, 'node', up)  9.95 us
    pallas_call x1, Pallas kernels, body(): pl.pallas_call(advance_kernel, grid=(QUANT,), in_specs=[SMEM, SMEM, SMEM,...  9.84 us
    all_to_all x1, starting transfers between devices, body(): lax.all_to_all(labels.reshape(owners, 1, LANES), 'dev', split_axis=0, con...  9.67 us
    all_to_all x1, waiting for transfers between devices, body(): lax.all_to_all(labels.reshape(owners, 1, LANES), 'dev', split_axis=0, con...  6.38 us
    pallas_call x1, Pallas kernels, body(): pl.pallas_call(arrange_kernel, grid=(QUANT,), in_specs=[SMEM, SMEM, VMEM,...  6.24 us
    ppermute x1, waiting for transfers between devices, body(): ghost_high = lax.ppermute(for_below, 'node', down)  5.5 us
    ppermute x1, starting transfers between devices, body(): low_tag = lax.ppermute(own, 'node', up)  5.11 us
  transfers between devices with their start and end apart: 6, of which 5 were waited for; matrix products, arithmetic and copies ran while one was open for 0% of the time, Pallas kernels for 4%

profile of v1, /device:TPU:449, one launch (start us, length us, event | category | flops | bytes accessed | tf_op | source)
XLA Modules:
  0.0 104.2 jit_solution(3329701380929253674)
XLA Ops:
  0.6 1.3 %label.1 = s32[32,128]{1,0:T(8,128)} custom-call(s32[1,1,16]{2,1,0:T(1,128)} %dest_ref.3, s32[1,1,16]{2,1,0:T(1,128)} %level_ref.1), custom_call_target="tpu_custom_call" | custom-call | tf_op jit(solution)/shard_map/label/pallas_call | solution.py:218
  1.9 9.7 %all-to-all-start = ((s32[32,1,128]{2,1,0:T(1,128)}), s32[32,1,128]{2,1,0:T(1,128)S(1)}, u32[]{:S(2)}, u32[]{:S(2)}) async-start(s32[32,1,128]{2,1,0:T(1,128)} %bitcast.11), calls=%async_computation | async-start | bytes 32768 | tf_op jit(solution)/shard_map/all_to_all | solution.py:225
  11.6 2.2 %pack.1 = bf16[32,7,16,256]{3,2,1,0:T(8,128)(2,1)} custom-call(s32[1,1,16]{2,1,0:T(1,128)} %dest_ref.3, bf16[16,7,16,256]{3,2,1,0:T(8,128)(2,1)} %bitcast.8), custom_call_target="tpu_custom_call" | custom-call | tf_op jit(solution)/shard_map/pack/pallas_call | solution.py:228
  13.8 6.4 %all-to-all-done = s32[32,1,128]{2,1,0:T(1,128)S(1)} async-done(((s32[32,1,128]{2,1,0:T(1,128)}), s32[32,1,128]{2,1,0:T(1,128)S(1)}, u32[]{:S(2)}, u32[]{:S(2)}) %all-to-all-start) | async-done | bytes 16416 | tf_op jit(solution)/shard_map/all_to_all | solution.py:225
  20.2 0.0 copy-start.3
  20.2 0.6 copy-done.3
  20.8 4.0 %all-to-all-start.1 = ((bf16[32,7,16,256]{3,2,1,0:T(8,128)(2,1)}), bf16[32,7,16,256]{3,2,1,0:T(8,128)(2,1)S(1)}, u32[]{:S(2)}, u32[]{:S(2)}) async-start(bf16[32,7,16,256]{3,2,1,0:T(8,128)(2,1)} %pack.1), calls=%async_computation.1 | async-start | bytes 3670016 | tf_op jit(solution)/shard_map/all_to_all | solution.py:236
  24.8 1.8 %rank.1 = (s32[32]{0:T(128)}, s32[1]{0:T(128)}, s32[32]{0:T(128)}, s32[32,128]{1,0:T(8,128)}) custom-call(s32[32,128]{1,0:T(8,128)} %bitcast.9, s32[32,128]{1,0:T(8,128)} %bitcast.10), custom_call_target="tpu_custom_call" | custom-call | tf_op jit(solution)/shard_map/rank/pallas_call | solution.py:237
  26.7 3.8 %collective-permute-start.1 = (s32[32,128]{1,0:T(8,128)}, s32[32,128]{1,0:T(8,128)S(1)}, u32[]{:S(2)}, u32[]{:S(2)}) collective-permute-start(s32[32,128]{1,0:T(8,128)} %get-tuple-element.11.own_ref), channel_id=1, source_target_pairs={{32,0},{64,32},{96,64},{128,96},{160,128},{192,160},{224,192},{256... | collective-permute-start | bytes 49160 | tf_op jit(solution)/shard_map/ppermute | solution.py:250
  30.5 5.1 %collective-permute-start = (s32[32,128]{1,0:T(8,128)}, s32[32,128]{1,0:T(8,128)S(1)}, u32[]{:S(2)}, u32[]{:S(2)}) collective-permute-start(s32[32,128]{1,0:T(8,128)} %get-tuple-element.11.own_ref), channel_id=1, source_target_pairs={{0,32},{32,64},{64,96},{96,128},{128,160},{160,192},{192,224},{224... | collective-permute-start | bytes 49160 | tf_op jit(solution)/shard_map/ppermute | solution.py:249
  35.6 0.0 collective-permute-done.1.high_ref
  35.7 0.0 copy-start.4
  35.7 1.0 collective-permute-done.low_ref
  36.7 0.0 copy-start.5
  36.7 29.4 %all-to-all-done.1.in_ref = bf16[32,7,16,256]{3,2,1,0:T(8,128)(2,1)S(1)} async-done(((bf16[32,7,16,256]{3,2,1,0:T(8,128)(2,1)}), bf16[32,7,16,256]{3,2,1,0:T(8,128)(2,1)S(1)}, u32[]{:S(2)}, u32[]{:S(2)}) %all-to-all-start.1) | async-done | bytes 1835040 | tf_op jit(solution)/shard_map/all_to_all | solution.py:236
  66.1 0.0 copy-start
  66.1 0.0 copy-done.4
  66.1 0.0 copy-done.5
  66.1 1.2 %copy-done = bf16[32,7,16,256]{3,2,1,0:T(8,128)(2,1)} copy-done((bf16[32,7,16,256]{3,2,1,0:T(8,128)(2,1)}, bf16[32,7,16,256]{3,2,1,0:T(8,128)(2,1)S(1)}, u32[]{:S(2)}) %copy-start) | copy-done | bytes 1835032
  67.4 6.2 %arrange.1 = (bf16[7,16,32,256]{3,2,1,0:T(8,128)(2,1)}, bf16[7,3,32,256]{3,2,1,0:T(8,128)(2,1)}, bf16[7,3,32,256]{3,2,1,0:T(8,128)(2,1)}) custom-call(s32[32]{0:T(128)} %get-tuple-element.10.source_ref, s32[1]{0:T(128)} %get-tuple-element.9.count_ref, s32[32,128]{1,0:T(8,128)} %get-tuple-element.11.own_ref, s32[32,128]{1,0:T(8,128)} %copy-done.5, ...), custom_call_target="tpu_custom_call" | custom-call | tf_op jit(solution)/shard_map/arrange/pallas_call | solution.py:255
  73.6 9.9 %collective-permute-start.2 = (bf16[7,3,32,256]{3,2,1,0:T(8,128)(2,1)}, bf16[7,3,32,256]{3,2,1,0:T(8,128)(2,1)S(1)}, u32[]{:S(2)}, u32[]{:S(2)}) collective-permute-start(bf16[7,3,32,256]{3,2,1,0:T(8,128)(2,1)} %get-tuple-element.13), channel_id=1, source_target_pairs={{0,32},{32,64},{64,96},{96,128},{128,160},{160,192},{192,224},{224... | collective-permute-start | bytes 1032200 | tf_op jit(solution)/shard_map/ppermute | solution.py:280
  83.6 1.9 %collective-permute-start.3 = (bf16[7,3,32,256]{3,2,1,0:T(8,128)(2,1)}, bf16[7,3,32,256]{3,2,1,0:T(8,128)(2,1)S(1)}, u32[]{:S(2)}, u32[]{:S(2)}) collective-permute-start(bf16[7,3,32,256]{3,2,1,0:T(8,128)(2,1)} %get-tuple-element.14), channel_id=1, source_target_pairs={{32,0},{64,32},{96,64},{128,96},{160,128},{192,160},{224,192},{256... | collective-permute-start | bytes 1032200 | tf_op jit(solution)/shard_map/ppermute | solution.py:279
  85.5 2.6 %collective-permute-done.2.low_ref = bf16[7,3,32,256]{3,2,1,0:T(8,128)(2,1)S(1)} collective-permute-done((bf16[7,3,32,256]{3,2,1,0:T(8,128)(2,1)}, bf16[7,3,32,256]{3,2,1,0:T(8,128)(2,1)S(1)}, u32[]{:S(2)}, u32[]{:S(2)}) %collective-permute-start.2) | collective-permute-done | bytes 344096 | tf_op jit(solution)/shard_map/ppermute | solution.py:280
  88.1 0.0 copy-start.1
  88.1 5.5 %collective-permute-done.3.high_ref = bf16[7,3,32,256]{3,2,1,0:T(8,128)(2,1)S(1)} collective-permute-done((bf16[7,3,32,256]{3,2,1,0:T(8,128)(2,1)}, bf16[7,3,32,256]{3,2,1,0:T(8,128)(2,1)S(1)}, u32[]{:S(2)}, u32[]{:S(2)}) %collective-permute-start.3) | collective-permute-done | bytes 344096 | tf_op jit(solution)/shard_map/ppermute | solution.py:279
  93.6 0.0 copy-start.2
  93.6 0.0 copy-done.1
  93.6 0.8 copy-done.2
  94.3 9.8 %advance.1 = bf16[32,7,16,256]{3,2,1,0:T(8,128)(2,1)} custom-call(f32[7]{0:T(128)} %speed_ref.1, f32[7]{0:T(128)} %limit_ref.1, s32[1]{0:T(128)} %get-tuple-element.9.count_ref, bf16[7,16,32,256]{3,2,1,0:T(8,128)(2,1)} %get-tuple-element.12.in_ref, bf16[7,3,32,256]{3,2,1,0:T(8,128)(2,1)} %copy-done.1, bf16[7,3,32,256]{3,2,1,0:T(8,128)(2,1)} %copy-done.2), custom_call_target="tpu_custom_call" | custom-call | tf_op jit(solution)/shard_map/advance/pallas_call | solution.py:281
Async XLA Ops:
  1.9 18.3 %all-to-all-start = ((s32[32,1,128]{2,1,0:T(1,128)}), s32[32,1,128]{2,1,0:T(1,128)S(1)}, u32[]{:S(2)}, u32[]{:S(2)}) async-start(s32[32,1,128]{2,1,0:T(1,128)} %bitcast.11), calls=%async_computation | async-start | bytes 32768 | tf_op jit(solution)/shard_map/all_to_all | solution.py:225
  20.2 0.6 copy-start.3
  20.8 45.3 %all-to-all-start.1 = ((bf16[32,7,16,256]{3,2,1,0:T(8,128)(2,1)}), bf16[32,7,16,256]{3,2,1,0:T(8,128)(2,1)S(1)}, u32[]{:S(2)}, u32[]{:S(2)}) async-start(bf16[32,7,16,256]{3,2,1,0:T(8,128)(2,1)} %pack.1), calls=%async_computation.1 | async-start | bytes 3670016 | tf_op jit(solution)/shard_map/all_to_all | solution.py:236
  26.7 9.0 %collective-permute-start.1 = (s32[32,128]{1,0:T(8,128)}, s32[32,128]{1,0:T(8,128)S(1)}, u32[]{:S(2)}, u32[]{:S(2)}) collective-permute-start(s32[32,128]{1,0:T(8,128)} %get-tuple-element.11.own_ref), channel_id=1, source_target_pairs={{32,0},{64,32},{96,64},{128,96},{160,128},{192,160},{224,192},{256... | collective-permute-start | bytes 49160 | tf_op jit(solution)/shard_map/ppermute | solution.py:250
  30.5 6.2 %collective-permute-start = (s32[32,128]{1,0:T(8,128)}, s32[32,128]{1,0:T(8,128)S(1)}, u32[]{:S(2)}, u32[]{:S(2)}) collective-permute-start(s32[32,128]{1,0:T(8,128)} %get-tuple-element.11.own_ref), channel_id=1, source_target_pairs={{0,32},{32,64},{64,96},{96,128},{128,160},{160,192},{192,224},{224... | collective-permute-start | bytes 49160 | tf_op jit(solution)/shard_map/ppermute | solution.py:249
  35.7 30.5 %copy-start.4 = (s32[32,128]{1,0:T(8,128)}, s32[32,128]{1,0:T(8,128)S(1)}, u32[]{:S(2)}) copy-start(s32[32,128]{1,0:T(8,128)S(1)} %collective-permute-done.1.high_ref) | copy-start | bytes 49156
  36.7 29.4 %copy-start.5 = (s32[32,128]{1,0:T(8,128)}, s32[32,128]{1,0:T(8,128)S(1)}, u32[]{:S(2)}) copy-start(s32[32,128]{1,0:T(8,128)S(1)} %collective-permute-done.low_ref) | copy-start | bytes 49156
  66.1 1.2 %copy-start = (bf16[32,7,16,256]{3,2,1,0:T(8,128)(2,1)}, bf16[32,7,16,256]{3,2,1,0:T(8,128)(2,1)S(1)}, u32[]{:S(2)}) copy-start(bf16[32,7,16,256]{3,2,1,0:T(8,128)(2,1)S(1)} %all-to-all-done.1.in_ref) | copy-start | bytes 5505028
  73.6 14.4 %collective-permute-start.2 = (bf16[7,3,32,256]{3,2,1,0:T(8,128)(2,1)}, bf16[7,3,32,256]{3,2,1,0:T(8,128)(2,1)S(1)}, u32[]{:S(2)}, u32[]{:S(2)}) collective-permute-start(bf16[7,3,32,256]{3,2,1,0:T(8,128)(2,1)} %get-tuple-element.13), channel_id=1, source_target_pairs={{0,32},{32,64},{64,96},{96,128},{128,160},{160,192},{192,224},{224... | collective-permute-start | bytes 1032200 | tf_op jit(solution)/shard_map/ppermute | solution.py:280
  83.6 10.0 %collective-permute-start.3 = (bf16[7,3,32,256]{3,2,1,0:T(8,128)(2,1)}, bf16[7,3,32,256]{3,2,1,0:T(8,128)(2,1)S(1)}, u32[]{:S(2)}, u32[]{:S(2)}) collective-permute-start(bf16[7,3,32,256]{3,2,1,0:T(8,128)(2,1)} %get-tuple-element.14), channel_id=1, source_target_pairs={{32,0},{64,32},{96,64},{128,96},{160,128},{192,160},{224,192},{256... | collective-permute-start | bytes 1032200 | tf_op jit(solution)/shard_map/ppermute | solution.py:279
  88.1 5.5 %copy-start.1 = (bf16[7,3,32,256]{3,2,1,0:T(8,128)(2,1)}, bf16[7,3,32,256]{3,2,1,0:T(8,128)(2,1)S(1)}, u32[]{:S(2)}) copy-start(bf16[7,3,32,256]{3,2,1,0:T(8,128)(2,1)S(1)} %collective-permute-done.2.low_ref) | copy-start | bytes 1032196
  93.6 0.8 copy-start.2

commit v2 on v0

v2 whole, which is shorter than its diff:
```python
import jax
import jax.numpy as jnp
from jax import lax
from jax.experimental import pallas as pl
from jax.experimental.pallas import tpu as pltpu
from jax.sharding import PartitionSpec as P

QUANT = 7
EDGE = 16
PLANE = EDGE * EDGE
SLOTS = 16
NEW_CAP = 32
LANES = 128
HALVES = PLANE // LANES
PITCH = EDGE + 1
GROUP = 16
HALF_TILES = QUANT * EDGE // 8
ROW_TILES = HALVES * HALF_TILES + 1
SENT = 5

COURANT = 0.4
WENO_EPS = 1e-06

SMEM = pl.BlockSpec(memory_space=pltpu.SMEM)
VMEM = pl.BlockSpec(memory_space=pltpu.VMEM)
ANY = pl.BlockSpec(memory_space=pl.ANY)


def pack_kernel(
    dest_ref, level_ref, blocks_ref, out_ref, work, tags, in_sems, out_sems, tag_sem
):
    loads = [
        pltpu.make_async_copy(blocks_ref.at[s], work.at[s], in_sems.at[s]) for s in range(SLOTS)
    ]
    for load in loads:
        load.start()
    row = lax.broadcasted_iota(jnp.int32, tags.shape, 0)
    values = jnp.zeros(tags.shape, jnp.int32)
    for s in range(SLOTS):
        values = jnp.where(row == dest_ref[0, 0, s], level_ref[0, 0, s] + 1, values)
    tags[...] = values.astype(jnp.float32).astype(jnp.bfloat16)
    stores = [pltpu.make_async_copy(tags, out_ref.at[:, ROW_TILES - 1], tag_sem)]
    stores[0].start()
    for s in range(SLOTS):
        loads[s].wait()
        for half in range(HALVES):
            store = pltpu.make_async_copy(
                work.at[s, :, :, half * LANES : (half + 1) * LANES],
                out_ref.at[dest_ref[0, 0, s], half * HALF_TILES : (half + 1) * HALF_TILES],
                out_sems.at[s, half],
            )
            store.start()
            stores.append(store)
    for store in stores:
        store.wait()


def rank_positions(in_ref, source, count_ref, new_ref, own_ref, tags_vm, tags_sm, sem):
    for i in range(NEW_CAP):
        tile = in_ref[i, ROW_TILES - 1].astype(jnp.float32)
        tags_vm[i : i + 1, :] = tile[0:1].astype(jnp.int32)
    copy = pltpu.make_async_copy(tags_vm, tags_sm, sem)
    copy.start()
    own_ref[...] = jnp.zeros_like(own_ref)
    for p in range(NEW_CAP):
        source[p] = 0
        new_ref[p] = -1
    copy.wait()
    count = jnp.int32(0)
    for i in range(NEW_CAP):
        tag = tags_sm[i, 0]
        here = tag > 0

        @pl.when(here)
        def _(i=i, tag=tag, count=count):
            source[count] = i
            new_ref[count] = tag - 1
            own_ref[pl.ds(count, 1), :] = tags_vm[pl.ds(i, 1), :]

        count = count + here.astype(jnp.int32)
    count_ref[0] = count
    return count


def arrange_kernel(
    in_ref, out_ref, below_ref, above_ref, own_ref, count_ref, new_ref,
    work, source, tags_vm, tags_sm, sem,
):
    count = rank_positions(in_ref, source, count_ref, new_ref, own_ref, tags_vm, tags_sm, sem)

    def quantity(q, carry):
        for half in range(HALVES):
            lanes = slice(half * LANES, (half + 1) * LANES)
            for p in range(NEW_CAP):
                for part in range(2):
                    tile = half * HALF_TILES + 2 * q + part
                    cells = in_ref[source[p], tile].astype(jnp.float32)
                    start = p * PITCH + part * 8
                    work[half, start : start + 8, :] = jnp.where(p < count, cells, 0.0)
            layers = []
            for c in range(EDGE):
                layer = work[half, pl.ds(c, NEW_CAP, stride=PITCH), :]
                out_ref[q, c, :, lanes] = layer.astype(jnp.bfloat16)
                layers.append(layer)
            for ref, near_layers in ((below_ref, layers), (above_ref, layers[::-1])):
                sent = list(near_layers[:3])
                sent.append(0.5 * (near_layers[2] + near_layers[3]))
                sent.append(0.5 * (near_layers[4] + near_layers[5]))
                for m, layer in enumerate(sent):
                    ref[SENT * q + m, :, lanes] = layer.astype(jnp.bfloat16)
        return carry

    lax.fori_loop(0, QUANT, quantity, 0)
    label = own_ref[...].astype(jnp.float32).astype(jnp.bfloat16)
    for half in range(HALVES):
        lanes = slice(half * LANES, (half + 1) * LANES)
        below_ref[SENT * QUANT, :, lanes] = label
        above_ref[SENT * QUANT, :, lanes] = label


def faces(read, first, last):
    cells, steps, bends, curves, turns = {}, {}, {}, {}, {}
    for k in range(first, last + 5):
        cells[k] = read(k)
        if k >= first + 1:
            steps[k] = cells[k] - cells[k - 1]
        if k >= first + 2:
            bends[k - 1] = 0.5 * (steps[k] - steps[k - 1])
            curves[k - 1] = (13.0 / 3.0) * (bends[k - 1] * bends[k - 1]) + WENO_EPS
        if k >= first + 3:
            turns[k - 1] = bends[k - 2] - bends[k - 1]
        if k >= first + 4:
            c = k - 2
            one = steps[c] + bends[c - 1]
            two = steps[c] + bends[c]
            three = steps[c + 1] - bends[c + 1]
            p_zero = curves[c - 1] + one * one
            p_one = curves[c] + two * two
            p_two = curves[c + 1] + three * three
            w_zero = p_one * p_two
            w_one = p_zero * p_two
            w_two = p_zero * p_one
            w_zero = w_zero * w_zero
            w_one = w_one * w_one
            w_two = 1.5 * (w_two * w_two)
            total = (w_zero + 6.0 * w_one) + (w_two + w_two)
            shift = (w_zero * turns[c] + w_two * turns[c + 1]) / total
            yield k - 4, 0.75 * (cells[c] + cells[c + 1]) + (shift - 0.5 * bends[c])


def tiles(body_of):
    def tile(index, carry):
        half = index % HALVES
        base = pl.multiple_of((index // HALVES) * GROUP, GROUP)
        body_of(base, pl.ds(base, GROUP), pl.ds(pl.multiple_of(half * LANES, LANES), LANES))
        return carry

    lax.fori_loop(0, HALVES * (NEW_CAP // GROUP), tile, 0)


def by_direction(speed_ref, q, run):
    @pl.when(speed_ref[q] >= 0.0)
    def _():
        run(q, True)

    @pl.when(speed_ref[q] < 0.0)
    def _():
        run(q, False)


def inner_kernel(speed_ref, in_ref, mid_ref):
    def run(q, forward):
        rate = (COURANT * 2.0 / 3.0) * jnp.abs(speed_ref[q])

        def tile(base, rows, lanes):
            def read(k):
                c = k - 3 if forward else EDGE + 2 - k
                return in_ref[q, c, rows, lanes].astype(jnp.float32)

            last = None
            for f, state in faces(read, 3, EDGE - 2):
                if f == 3:
                    mid_ref[q, 0, rows, lanes] = state
                else:
                    mid_ref[q, f - 3, rows, lanes] = read(f + 2) - rate * (state - last)
                last = state
            mid_ref[q, EDGE - 4, rows, lanes] = last

        tiles(tile)

    def quantity(q, carry):
        by_direction(speed_ref, q, run)
        return carry

    lax.fori_loop(0, QUANT, quantity, 0)


def outer_kernel(
    speed_ref, limit_ref, count_ref, own_ref, in_ref, mid_ref, low_ref, high_ref, out_ref,
    done, work, sems,
):
    count = count_ref[0]

    def run(q, forward):
        limit = limit_ref[q]
        rate = (COURANT * 2.0 / 3.0) * jnp.abs(speed_ref[q])

        def tile(base, rows, lanes):
            own = own_ref[rows, :].astype(jnp.float32)

            def ghosts(ref):
                sent = [
                    ref[SENT * q + m, rows, lanes].astype(jnp.float32) for m in range(SENT)
                ]
                mean = (0.5 * (sent[0] + sent[1])).astype(jnp.bfloat16).astype(jnp.float32)
                tag = ref[SENT * QUANT, rows, lanes].astype(jnp.float32)
                finer = tag > own
                coarser = tag < own
                return [
                    jnp.where(finer, fine, jnp.where(coarser, coarse, same))
                    for fine, coarse, same in (
                        (mean, sent[0], sent[0]),
                        (sent[3], sent[0], sent[1]),
                        (sent[4], sent[1], sent[2]),
                    )
                ]

            before, after = (low_ref, high_ref) if forward else (high_ref, low_ref)
            before = ghosts(before)
            after = ghosts(after)

            def read(k):
                if k < 3:
                    return before[2 - k]
                if k >= EDGE + 3:
                    return after[k - EDGE - 3]
                c = k - 3 if forward else EDGE + 2 - k
                return in_ref[q, c, rows, lanes].astype(jnp.float32)

            def cell(k):
                return k if forward else EDGE - 1 - k

            advanced = {}
            last = None
            for f, state in faces(read, 0, 2):
                if f >= 1:
                    advanced[cell(f - 1)] = read(f + 2) - rate * (state - last)
                last = state
            advanced[cell(2)] = read(5) - rate * (mid_ref[q, 0, rows, lanes] - last)
            last = mid_ref[q, EDGE - 4, rows, lanes]
            for f, state in faces(read, EDGE - 1, EDGE):
                advanced[cell(f - 1)] = read(f + 2) - rate * (state - last)
                last = state
            for k in range(3, EDGE - 2):
                advanced[cell(k)] = mid_ref[q, k - 2, rows, lanes]
            for c in range(EDGE):
                value = advanced[c]
                if c % 2 == 1:
                    guess = advanced[c - 1]
                    if c < EDGE - 1:
                        guess = 0.5 * (guess + advanced[c + 1])
                    detail = value - guess
                    value = guess + detail - jnp.clip(detail, -limit, limit)
                work[pl.ds(c, GROUP, stride=PITCH), :] = value
            for p in range(GROUP):
                cells = work[p * PITCH : p * PITCH + EDGE, :]
                cells = jnp.where(base + p < count, cells, 0.0)
                done[q, base + p, :, lanes] = cells.astype(jnp.bfloat16)

        tiles(tile)

    def copy(q):
        return pltpu.make_async_copy(done.at[q], out_ref.at[:, q], sems.at[q])

    def quantity(q, carry):
        by_direction(speed_ref, q, run)
        copy(q).start()
        return carry

    lax.fori_loop(0, QUANT, quantity, 0)
    for q in range(QUANT):
        copy(q).wait()


PARAMS = pltpu.CompilerParams(vmem_limit_bytes=24 << 20)


def far(value):
    return pltpu.with_memory_space_constraint(value, pltpu.HBM)


def near(value):
    return pltpu.with_memory_space_constraint(value, pltpu.VMEM)


def struct(shape, dtype):
    return jax.ShapeDtypeStruct(shape, dtype)


def body(blocks, levels, destinations, speeds, thresholds):
    owners = lax.axis_size("dev")
    count = lax.axis_size("node")
    up = [(i, i + 1) for i in range(count - 1)]
    down = [(i + 1, i) for i in range(count - 1)]
    row = (owners, ROW_TILES, 8, LANES)
    outgoing = pl.pallas_call(
        pack_kernel,
        in_specs=[SMEM, SMEM, ANY],
        out_specs=ANY,
        out_shape=pltpu.HBM(row, jnp.bfloat16),
        scratch_shapes=[
            pltpu.VMEM((SLOTS, HALF_TILES, 8, PLANE), jnp.bfloat16),
            pltpu.VMEM((owners, 8, LANES), jnp.bfloat16),
            pltpu.SemaphoreType.DMA((SLOTS,)),
            pltpu.SemaphoreType.DMA((SLOTS, HALVES)),
            pltpu.SemaphoreType.DMA,
        ],
        compiler_params=PARAMS,
        name="pack",
    )(far(destinations), far(levels), far(blocks.reshape(SLOTS, HALF_TILES, 8, PLANE)))
    incoming = lax.all_to_all(outgoing, "dev", split_axis=0, concat_axis=0, tiled=True)
    sent = struct((SENT * QUANT + 1, NEW_CAP, PLANE), jnp.bfloat16)
    arranged, for_below, for_above, own, total, new_levels = pl.pallas_call(
        arrange_kernel,
        in_specs=[VMEM],
        out_specs=(VMEM, VMEM, VMEM, VMEM, SMEM, SMEM),
        out_shape=(
            pltpu.VMEM((QUANT, EDGE, NEW_CAP, PLANE), jnp.bfloat16),
            sent,
            sent,
            pltpu.VMEM((NEW_CAP, LANES), jnp.int32),
            struct((1,), jnp.int32),
            struct((NEW_CAP,), jnp.int32),
        ),
        scratch_shapes=[
            pltpu.VMEM((HALVES, NEW_CAP * PITCH + 8, LANES), jnp.float32),
            pltpu.SMEM((NEW_CAP,), jnp.int32),
            pltpu.VMEM((owners, LANES), jnp.int32),
            pltpu.SMEM((owners, LANES), jnp.int32),
            pltpu.SemaphoreType.DMA,
        ],
        compiler_params=PARAMS,
        name="arrange",
    )(near(incoming))
    ghost_high = lax.ppermute(for_below, "node", down)
    ghost_low = lax.ppermute(for_above, "node", up)
    inner = pl.pallas_call(
        inner_kernel,
        in_specs=[SMEM, VMEM],
        out_specs=VMEM,
        out_shape=pltpu.VMEM((QUANT, EDGE - 3, NEW_CAP, PLANE), jnp.float32),
        compiler_params=PARAMS,
        cost_estimate=pl.CostEstimate(
            flops=40 * QUANT * EDGE * NEW_CAP * PLANE, transcendentals=0, bytes_accessed=0
        ),
        name="inner",
    )(speeds, near(arranged))
    updated = pl.pallas_call(
        outer_kernel,
        in_specs=[SMEM, SMEM, SMEM, VMEM, VMEM, VMEM, VMEM, VMEM],
        out_specs=ANY,
        out_shape=struct((NEW_CAP, QUANT, EDGE, PLANE), jnp.bfloat16),
        scratch_shapes=[
            pltpu.VMEM((QUANT, NEW_CAP, EDGE, PLANE), jnp.bfloat16),
            pltpu.VMEM((GROUP * PITCH + 8, LANES), jnp.float32),
            pltpu.SemaphoreType.DMA((QUANT,)),
        ],
        compiler_params=PARAMS,
        name="outer",
    )(
        speeds, thresholds, total, near(own), near(arranged), near(inner),
        near(ghost_low), near(ghost_high),
    )
    return (
        updated.reshape(1, 1, NEW_CAP, QUANT, EDGE, PLANE),
        new_levels.reshape(1, 1, NEW_CAP),
    )


def solution(mesh):
    return jax.shard_map(
        body,
        mesh=mesh,
        in_specs=(
            P("node", "dev", None, None, None, None),
            P("node", "dev", None),
            P("node", "dev", None),
            P(),
            P(),
        ),
        out_specs=(P("node", "dev", None, None, None, None), P("node", "dev", None)),
        check_vma=False,
    )
```

time: 176 us -> 87 us (0.49)
  the two profiles are of different devices: /device:TPU:195 before, /device:TPU:449 now
where the time goes in v2:
time: 87 us; the launch traced here: 86.7 us
  blocking collectives  54.4 us (63%)
  Pallas kernels  16.1 us (19%)
  starting transfers between devices  10.1 us (12%)
  waiting for transfers between devices  5.37 us (6%)
    all_to_all x1, blocking collectives, body(): lax.all_to_all(outgoing, 'dev', split_axis=0, concat_axis=0, tiled=True)  54.4 us
    ppermute x1, starting transfers between devices, body(): ghost_low = lax.ppermute(for_above, 'node', up)  8.22 us
    ppermute x1, waiting for transfers between devices, body(): ghost_high = lax.ppermute(for_below, 'node', down)  5.37 us
    pallas_call x1, Pallas kernels, body(): pl.pallas_call(outer_kernel, in_specs=[SMEM, SMEM, SMEM, VMEM, VMEM, VMEM...  5.17 us
    pallas_call x1, Pallas kernels, body(): pl.pallas_call(inner_kernel, in_specs=[SMEM, VMEM], out_specs=VMEM, out_s...  5.07 us
    pallas_call x1, Pallas kernels, body(): pl.pallas_call(pack_kernel, in_specs=[SMEM, SMEM, ANY], out_specs=ANY, ou...  2.99 us
    pallas_call x1, Pallas kernels, body(): pl.pallas_call(arrange_kernel, in_specs=[VMEM], out_specs=(VMEM, VMEM, VM...  2.83 us
    ppermute x1, starting transfers between devices, body(): ghost_high = lax.ppermute(for_below, 'node', down)  1.92 us
  transfers between devices with their start and end apart: 2, of which 1 were waited for; matrix products, arithmetic and copies ran while one was open for 0% of the time, Pallas kernels for 6%

profile of v2, /device:TPU:449, one launch (start us, length us, event | category | flops | bytes accessed | tf_op | source)
XLA Modules:
  0.0 86.7 jit_solution(6070973681603224069)
XLA Ops:
  0.6 3.0 %pack.1 = bf16[32,29,8,128]{3,2,1,0:T(8,128)(2,1)} custom-call(s32[1,1,16]{2,1,0:T(1,128)} %dest_ref.1, s32[1,1,16]{2,1,0:T(1,128)} %level_ref.1, bf16[16,14,8,256]{3,2,1,0:T(8,128)(2,1)} %bitcast.4), custom_call_target="tpu_custom_call" | custom-call | tf_op jit(solution)/shard_map/pack/pallas_call | solution.py:306
  3.6 54.4 %all_to_all.5.in_ref = bf16[32,29,8,128]{3,2,1,0:T(8,128)(2,1)S(1)} all-to-all(bf16[32,29,8,128]{3,2,1,0:T(8,128)(2,1)} %pack.1), channel_id=1, replica_groups=mesh['node'=32,'dev'=32] {'dev'}, dimensions={0} | all-to-all | bytes 3801088 | tf_op jit(solution)/shard_map/all_to_all | solution.py:321
  58.1 0.0 copy-start
  58.1 2.8 %arrange.1 = (bf16[7,16,32,256]{3,2,1,0:T(8,128)(2,1)S(1)}, bf16[36,32,256]{2,1,0:T(8,128)(2,1)S(1)}, bf16[36,32,256]{2,1,0:T(8,128)(2,1)S(1)}, s32[32,128]{1,0:T(8,128)S(1)}, s32[1]{0:T(128)}, /*index=5*/s32[32]{0:T(128)}) custom-call(bf16[32,29,8,128]{3,2,1,0:T(8,128)(2,1)S(1)} %all_to_all.5.in_ref), custom_call_target="tpu_custom_call" | custom-call | tf_op jit(solution)/shard_map/arrange/pallas_call | solution.py:323
  60.9 8.2 %collective-permute-start = (bf16[36,32,256]{2,1,0:T(8,128)(2,1)S(1)}, bf16[36,32,256]{2,1,0:T(8,128)(2,1)S(1)}, u32[]{:S(2)}, u32[]{:S(2)}) collective-permute-start(bf16[36,32,256]{2,1,0:T(8,128)(2,1)S(1)} %get-tuple-element.11), channel_id=1, source_target_pairs={{0,32},{32,64},{64,96},{96,128},{128,160},{160,192},{192,224},{224... | collective-permute-start | bytes 1769480 | tf_op jit(solution)/shard_map/ppermute | solution.py:346
  69.1 1.9 %collective-permute-start.1 = (bf16[36,32,256]{2,1,0:T(8,128)(2,1)S(1)}, bf16[36,32,256]{2,1,0:T(8,128)(2,1)S(1)}, u32[]{:S(2)}, u32[]{:S(2)}) collective-permute-start(bf16[36,32,256]{2,1,0:T(8,128)(2,1)S(1)} %get-tuple-element.12), channel_id=1, source_target_pairs={{32,0},{64,32},{96,64},{128,96},{160,128},{192,160},{224,192},{256... | collective-permute-start | bytes 1769480 | tf_op jit(solution)/shard_map/ppermute | solution.py:345
  71.0 0.0 copy-done
  71.1 0.0 copy-start.1
  71.1 5.1 %inner.1.mid_ref = f32[7,13,32,256]{3,2,1,0:T(8,128)S(1)} custom-call(f32[7]{0:T(128)S(1)} %copy-done, bf16[7,16,32,256]{3,2,1,0:T(8,128)(2,1)S(1)} %get-tuple-element.10.in_ref), custom_call_target="tpu_custom_call" | custom-call | flops 36700160 | tf_op jit(solution)/shard_map/inner/pallas_call | solution.py:347
  76.2 0.0 collective-permute-done.low_ref
  76.2 5.4 %collective-permute-done.1.high_ref = bf16[36,32,256]{2,1,0:T(8,128)(2,1)S(1)} collective-permute-done((bf16[36,32,256]{2,1,0:T(8,128)(2,1)S(1)}, bf16[36,32,256]{2,1,0:T(8,128)(2,1)S(1)}, u32[]{:S(2)}, u32[]{:S(2)}) %collective-permute-start.1) | collective-permute-done | bytes 589856 | tf_op jit(solution)/shard_map/ppermute | solution.py:345
  81.5 0.0 copy-done.1
  81.5 5.2 %outer.1 = bf16[32,7,16,256]{3,2,1,0:T(8,128)(2,1)} custom-call(f32[7]{0:T(128)S(1)} %copy-done, f32[7]{0:T(128)S(1)} %copy-done.1, s32[1]{0:T(128)} %get-tuple-element.8.count_ref, s32[32,128]{1,0:T(8,128)S(1)} %get-tuple-element.9.own_ref, bf16[7,16,32,256]{3,2,1,0:T(8,128)(2,1)S(1)} %get-tuple-element.10.in_ref, f32[7,13,32,256]{3,2,1,0:T(8,128)S(1)} %inner.1.mid_ref, ...), custom_call_target="tpu_custom_call" | custom-call | tf_op jit(solution)/shard_map/outer/pallas_call | solution.py:358
Async XLA Ops:
  58.1 13.0 %copy-start = (f32[7]{0:T(128)S(1)}, f32[7]{0:T(128)}, u32[]{:S(2)}) copy-start(f32[7]{0:T(128)} %speed_ref.3) | copy-start | bytes 88
  60.9 15.3 %collective-permute-start = (bf16[36,32,256]{2,1,0:T(8,128)(2,1)S(1)}, bf16[36,32,256]{2,1,0:T(8,128)(2,1)S(1)}, u32[]{:S(2)}, u32[]{:S(2)}) collective-permute-start(bf16[36,32,256]{2,1,0:T(8,128)(2,1)S(1)} %get-tuple-element.11), channel_id=1, source_target_pairs={{0,32},{32,64},{64,96},{96,128},{128,160},{160,192},{192,224},{224... | collective-permute-start | bytes 1769480 | tf_op jit(solution)/shard_map/ppermute | solution.py:346
  69.1 12.4 %collective-permute-start.1 = (bf16[36,32,256]{2,1,0:T(8,128)(2,1)S(1)}, bf16[36,32,256]{2,1,0:T(8,128)(2,1)S(1)}, u32[]{:S(2)}, u32[]{:S(2)}) collective-permute-start(bf16[36,32,256]{2,1,0:T(8,128)(2,1)S(1)} %get-tuple-element.12), channel_id=1, source_target_pairs={{32,0},{64,32},{96,64},{128,96},{160,128},{192,160},{224,192},{256... | collective-permute-start | bytes 1769480 | tf_op jit(solution)/shard_map/ppermute | solution.py:345
  71.1 10.5 %copy-start.1 = (f32[7]{0:T(128)S(1)}, f32[7]{0:T(128)}, u32[]{:S(2)}) copy-start(f32[7]{0:T(128)} %limit_ref.1) | copy-start | bytes 88

commit v3 on v2

--- a/solution.py
+++ b/solution.py
@@ -1,3 +1,5 @@
+import functools
+
 import jax
 import jax.numpy as jnp
 from jax import lax
@@ -26,33 +28,24 @@
 ANY = pl.BlockSpec(memory_space=pl.ANY)
 
 
-def pack_kernel(
-    dest_ref, level_ref, blocks_ref, out_ref, work, tags, in_sems, out_sems, tag_sem
-):
-    loads = [
-        pltpu.make_async_copy(blocks_ref.at[s], work.at[s], in_sems.at[s]) for s in range(SLOTS)
-    ]
-    for load in loads:
-        load.start()
-    row = lax.broadcasted_iota(jnp.int32, tags.shape, 0)
-    values = jnp.zeros(tags.shape, jnp.int32)
+def pack_kernel(dest_ref, level_ref, blocks_ref, out_ref, sems):
+    last = ROW_TILES - 1
+    out_ref[:, last] = jnp.zeros((out_ref.shape[0], 8, LANES), jnp.bfloat16)
     for s in range(SLOTS):
-        values = jnp.where(row == dest_ref[0, 0, s], level_ref[0, 0, s] + 1, values)
-    tags[...] = values.astype(jnp.float32).astype(jnp.bfloat16)
-    stores = [pltpu.make_async_copy(tags, out_ref.at[:, ROW_TILES - 1], tag_sem)]
-    stores[0].start()
+        tag = (level_ref[0, 0, s] + 1).astype(jnp.float32)
+        out_ref[dest_ref[0, 0, s], last] = jnp.full((8, LANES), tag).astype(jnp.bfloat16)
+    copies = []
     for s in range(SLOTS):
-        loads[s].wait()
         for half in range(HALVES):
-            store = pltpu.make_async_copy(
-                work.at[s, :, :, half * LANES : (half + 1) * LANES],
+            copy = pltpu.make_async_copy(
+                blocks_ref.at[s, :, :, half * LANES : (half + 1) * LANES],
                 out_ref.at[dest_ref[0, 0, s], half * HALF_TILES : (half + 1) * HALF_TILES],
-                out_sems.at[s, half],
+                sems.at[s, half],
             )
-            store.start()
-            stores.append(store)
-    for store in stores:
-        store.wait()
+            copy.start()
+            copies.append(copy)
+    for copy in copies:
+        copy.wait()
 
 
 def rank_positions(in_ref, source, count_ref, new_ref, own_ref, tags_vm, tags_sm, sem):
@@ -82,11 +75,19 @@
     return count
 
 
+def outward(layers):
+    sent = list(layers[:3])
+    sent.append(0.5 * (layers[2] + layers[3]))
+    sent.append(0.5 * (layers[4] + layers[5]))
+    return [layer.astype(jnp.bfloat16) for layer in sent]
+
+
 def arrange_kernel(
-    in_ref, out_ref, below_ref, above_ref, own_ref, count_ref, new_ref,
+    in_ref, out_ref, link_ref, chip_ref, own_ref, count_ref, new_ref,
     work, source, tags_vm, tags_sm, sem,
 ):
     count = rank_positions(in_ref, source, count_ref, new_ref, own_ref, tags_vm, tags_sm, sem)
+    even = lax.axis_index("node") % 2 == 0
 
     def quantity(q, carry):
         for half in range(HALVES):
@@ -102,20 +103,18 @@
                 layer = work[half, pl.ds(c, NEW_CAP, stride=PITCH), :]
                 out_ref[q, c, :, lanes] = layer.astype(jnp.bfloat16)
                 layers.append(layer)
-            for ref, near_layers in ((below_ref, layers), (above_ref, layers[::-1])):
-                sent = list(near_layers[:3])
-                sent.append(0.5 * (near_layers[2] + near_layers[3]))
-                sent.append(0.5 * (near_layers[4] + near_layers[5]))
-                for m, layer in enumerate(sent):
-                    ref[SENT * q + m, :, lanes] = layer.astype(jnp.bfloat16)
+            bottom, top = outward(layers), outward(layers[::-1])
+            for m in range(SENT):
+                link_ref[SENT * q + m, :, lanes] = jnp.where(even, bottom[m], top[m])
+                chip_ref[SENT * q + m, :, lanes] = jnp.where(even, top[m], bottom[m])
         return carry
 
     lax.fori_loop(0, QUANT, quantity, 0)
     label = own_ref[...].astype(jnp.float32).astype(jnp.bfloat16)
     for half in range(HALVES):
         lanes = slice(half * LANES, (half + 1) * LANES)
-        below_ref[SENT * QUANT, :, lanes] = label
-        above_ref[SENT * QUANT, :, lanes] = label
+        link_ref[SENT * QUANT, :, lanes] = label
+        chip_ref[SENT * QUANT, :, lanes] = label
 
 
 def faces(read, first, last):
@@ -196,12 +195,13 @@
 
 
 def outer_kernel(
-    speed_ref, limit_ref, count_ref, own_ref, in_ref, mid_ref, low_ref, high_ref, out_ref,
+    speed_ref, limit_ref, count_ref, own_ref, in_ref, mid_ref, link_ref, chip_ref, out_ref,
     done, work, sems,
 ):
     count = count_ref[0]
-
-    def run(q, forward):
+    even = lax.axis_index("node") % 2 == 0
+
+    def run(q, forward, link_first):
         limit = limit_ref[q]
         rate = (COURANT * 2.0 / 3.0) * jnp.abs(speed_ref[q])
 
@@ -225,7 +225,7 @@
                     )
                 ]
 
-            before, after = (low_ref, high_ref) if forward else (high_ref, low_ref)
+            before, after = (link_ref, chip_ref) if link_first else (chip_ref, link_ref)
             before = ghosts(before)
             after = ghosts(after)
 
@@ -273,7 +273,11 @@
         return pltpu.make_async_copy(done.at[q], out_ref.at[:, q], sems.at[q])
 
     def quantity(q, carry):
-        by_direction(speed_ref, q, run)
+        for link_first in (True, False):
+            @pl.when((even == (speed_ref[q] >= 0.0)) == link_first)
+            def _(link_first=link_first):
+                by_direction(speed_ref, q, functools.partial(run, link_first=link_first))
+
         copy(q).start()
         return carry
 
@@ -297,30 +301,27 @@
     return jax.ShapeDtypeStruct(shape, dtype)
 
 
+def swaps(start, count):
+    lower = range(start, count - 1, 2)
+    return [(i, i + 1) for i in lower] + [(i + 1, i) for i in lower]
+
+
 def body(blocks, levels, destinations, speeds, thresholds):
     owners = lax.axis_size("dev")
     count = lax.axis_size("node")
-    up = [(i, i + 1) for i in range(count - 1)]
-    down = [(i + 1, i) for i in range(count - 1)]
     row = (owners, ROW_TILES, 8, LANES)
     outgoing = pl.pallas_call(
         pack_kernel,
         in_specs=[SMEM, SMEM, ANY],
-        out_specs=ANY,
-        out_shape=pltpu.HBM(row, jnp.bfloat16),
-        scratch_shapes=[
-            pltpu.VMEM((SLOTS, HALF_TILES, 8, PLANE), jnp.bfloat16),
-            pltpu.VMEM((owners, 8, LANES), jnp.bfloat16),
-            pltpu.SemaphoreType.DMA((SLOTS,)),
-            pltpu.SemaphoreType.DMA((SLOTS, HALVES)),
-            pltpu.SemaphoreType.DMA,
-        ],
+        out_specs=VMEM,
+        out_shape=pltpu.VMEM(row, jnp.bfloat16),
+        scratch_shapes=[pltpu.SemaphoreType.DMA((SLOTS, HALVES))],
         compiler_params=PARAMS,
         name="pack",
     )(far(destinations), far(levels), far(blocks.reshape(SLOTS, HALF_TILES, 8, PLANE)))
     incoming = lax.all_to_all(outgoing, "dev", split_axis=0, concat_axis=0, tiled=True)
     sent = struct((SENT * QUANT + 1, NEW_CAP, PLANE), jnp.bfloat16)
-    arranged, for_below, for_above, own, total, new_levels = pl.pallas_call(
+    arranged, for_link, for_chip, own, total, new_levels = pl.pallas_call(
         arrange_kernel,
         in_specs=[VMEM],
         out_specs=(VMEM, VMEM, VMEM, VMEM, SMEM, SMEM),
@@ -342,8 +343,8 @@
         compiler_params=PARAMS,
         name="arrange",
     )(near(incoming))
-    ghost_high = lax.ppermute(for_below, "node", down)
-    ghost_low = lax.ppermute(for_above, "node", up)
+    from_link = lax.ppermute(for_link, "node", swaps(1, count))
+    from_chip = lax.ppermute(for_chip, "node", swaps(0, count))
     inner = pl.pallas_call(
         inner_kernel,
         in_specs=[SMEM, VMEM],
@@ -369,7 +370,7 @@
         name="outer",
     )(
         speeds, thresholds, total, near(own), near(arranged), near(inner),
-        near(ghost_low), near(ghost_high),
+        near(from_link), near(from_chip),
     )
     return (
         updated.reshape(1, 1, NEW_CAP, QUANT, EDGE, PLANE),

time: 87 us -> 81.3 us (0.934)
  waiting for transfers between devices: 5.37 us -> 0.52 us
    ppermute x2, waiting for transfers between devices: 5.37 us -> 0.52 us  [the longest x1 0.52 us: body(): from_link = lax.ppermute(for_link, 'node', swaps(1, count))]
    pallas_call x1, Pallas kernels: 2.99 us -> 2.12 us  [body(): pl.pallas_call(pack_kernel, in_specs=[SMEM, SMEM, ANY], out_specs=VMEM, o...]
where the time goes in v3:
time: 81.3 us; the launch traced here: 81 us
  blocking collectives  54.2 us (67%)
  Pallas kernels  15.4 us (19%)
  starting transfers between devices  10.1 us (12%)
    all_to_all x1, blocking collectives, body(): lax.all_to_all(outgoing, 'dev', split_axis=0, concat_axis=0, tiled=True)  54.2 us
    ppermute x1, starting transfers between devices, body(): from_link = lax.ppermute(for_link, 'node', swaps(1, count))  8.23 us
    pallas_call x1, Pallas kernels, body(): pl.pallas_call(outer_kernel, in_specs=[SMEM, SMEM, SMEM, VMEM, VMEM, VMEM...  5.33 us
    pallas_call x1, Pallas kernels, body(): pl.pallas_call(inner_kernel, in_specs=[SMEM, VMEM], out_specs=VMEM, out_s...  5.07 us
    pallas_call x1, Pallas kernels, body(): pl.pallas_call(arrange_kernel, in_specs=[VMEM], out_specs=(VMEM, VMEM, VM...  2.9 us
    pallas_call x1, Pallas kernels, body(): pl.pallas_call(pack_kernel, in_specs=[SMEM, SMEM, ANY], out_specs=VMEM, o...  2.12 us
    ppermute x1, starting transfers between devices, body(): from_chip = lax.ppermute(for_chip, 'node', swaps(0, count))  1.92 us
  transfers between devices with their start and end apart: 2, of which 1 were waited for; matrix products, arithmetic and copies ran while one was open for 0% of the time, Pallas kernels for 6%

profile of v3, /device:TPU:449, one launch (start us, length us, event | category | flops | bytes accessed | tf_op | source)
XLA Modules:
  0.0 81.0 jit_solution(9317068758182409468)
XLA Ops:
  0.6 2.1 %pack.1 = bf16[32,29,8,128]{3,2,1,0:T(8,128)(2,1)S(1)} custom-call(s32[1,1,16]{2,1,0:T(1,128)} %dest_ref.1, s32[1,1,16]{2,1,0:T(1,128)} %level_ref.1, bf16[16,14,8,256]{3,2,1,0:T(8,128)(2,1)} %bitcast.4), custom_call_target="tpu_custom_call" | custom-call | tf_op jit(solution)/shard_map/pack/pallas_call | solution.py:313
  2.8 54.2 %all_to_all.5.in_ref = bf16[32,29,8,128]{3,2,1,0:T(8,128)(2,1)S(1)} all-to-all(bf16[32,29,8,128]{3,2,1,0:T(8,128)(2,1)S(1)} %pack.1), channel_id=1, replica_groups=mesh['node'=32,'dev'=32] {'dev'}, dimensions={0} | all-to-all | bytes 3801088 | tf_op jit(solution)/shard_map/all_to_all | solution.py:322
  57.0 0.0 copy-start
  57.0 2.9 %arrange.1 = (bf16[7,16,32,256]{3,2,1,0:T(8,128)(2,1)S(1)}, bf16[36,32,256]{2,1,0:T(8,128)(2,1)S(1)}, bf16[36,32,256]{2,1,0:T(8,128)(2,1)S(1)}, s32[32,128]{1,0:T(8,128)S(1)}, s32[1]{0:T(128)}, /*index=5*/s32[32]{0:T(128)}) custom-call(bf16[32,29,8,128]{3,2,1,0:T(8,128)(2,1)S(1)} %all_to_all.5.in_ref), custom_call_target="tpu_custom_call" | custom-call | tf_op jit(solution)/shard_map/arrange/pallas_call | solution.py:324
  59.9 8.2 %collective-permute-start = (bf16[36,32,256]{2,1,0:T(8,128)(2,1)S(1)}, bf16[36,32,256]{2,1,0:T(8,128)(2,1)S(1)}, u32[]{:S(2)}, u32[]{:S(2)}) collective-permute-start(bf16[36,32,256]{2,1,0:T(8,128)(2,1)S(1)} %get-tuple-element.11), channel_id=1, source_target_pairs={{32,64},{96,128},{160,192},{224,256},{288,320},{352,384},{416,448}... | collective-permute-start | bytes 1769480 | tf_op jit(solution)/shard_map/ppermute | solution.py:346
  68.1 1.9 %collective-permute-start.1 = (bf16[36,32,256]{2,1,0:T(8,128)(2,1)S(1)}, bf16[36,32,256]{2,1,0:T(8,128)(2,1)S(1)}, u32[]{:S(2)}, u32[]{:S(2)}) collective-permute-start(bf16[36,32,256]{2,1,0:T(8,128)(2,1)S(1)} %get-tuple-element.12), channel_id=1, source_target_pairs={{0,32},{64,96},{128,160},{192,224},{256,288},{320,352},{384,416},{... | collective-permute-start | bytes 1769480 | tf_op jit(solution)/shard_map/ppermute | solution.py:347
  70.1 0.0 copy-done
  70.1 0.0 copy-start.1
  70.1 5.1 %inner.1.mid_ref = f32[7,13,32,256]{3,2,1,0:T(8,128)S(1)} custom-call(f32[7]{0:T(128)S(1)} %copy-done, bf16[7,16,32,256]{3,2,1,0:T(8,128)(2,1)S(1)} %get-tuple-element.10.in_ref), custom_call_target="tpu_custom_call" | custom-call | flops 36700160 | tf_op jit(solution)/shard_map/inner/pallas_call | solution.py:348
  75.2 0.5 collective-permute-done.link_ref
  75.7 0.0 collective-permute-done.1.chip_ref
  75.7 0.0 copy-done.1
  75.7 5.3 %outer.1 = bf16[32,7,16,256]{3,2,1,0:T(8,128)(2,1)} custom-call(f32[7]{0:T(128)S(1)} %copy-done, f32[7]{0:T(128)S(1)} %copy-done.1, s32[1]{0:T(128)} %get-tuple-element.8.count_ref, s32[32,128]{1,0:T(8,128)S(1)} %get-tuple-element.9.own_ref, bf16[7,16,32,256]{3,2,1,0:T(8,128)(2,1)S(1)} %get-tuple-element.10.in_ref, f32[7,13,32,256]{3,2,1,0:T(8,128)S(1)} %inner.1.mid_ref, ...), custom_call_target="tpu_custom_call" | custom-call | tf_op jit(solution)/shard_map/outer/pallas_call | solution.py:359
Async XLA Ops:
  57.0 13.1 %copy-start = (f32[7]{0:T(128)S(1)}, f32[7]{0:T(128)}, u32[]{:S(2)}) copy-start(f32[7]{0:T(128)} %speed_ref.3) | copy-start | bytes 88
  59.9 15.8 %collective-permute-start = (bf16[36,32,256]{2,1,0:T(8,128)(2,1)S(1)}, bf16[36,32,256]{2,1,0:T(8,128)(2,1)S(1)}, u32[]{:S(2)}, u32[]{:S(2)}) collective-permute-start(bf16[36,32,256]{2,1,0:T(8,128)(2,1)S(1)} %get-tuple-element.11), channel_id=1, source_target_pairs={{32,64},{96,128},{160,192},{224,256},{288,320},{352,384},{416,448}... | collective-permute-start | bytes 1769480 | tf_op jit(solution)/shard_map/ppermute | solution.py:346
  68.1 7.6 %collective-permute-start.1 = (bf16[36,32,256]{2,1,0:T(8,128)(2,1)S(1)}, bf16[36,32,256]{2,1,0:T(8,128)(2,1)S(1)}, u32[]{:S(2)}, u32[]{:S(2)}) collective-permute-start(bf16[36,32,256]{2,1,0:T(8,128)(2,1)S(1)} %get-tuple-element.12), channel_id=1, source_target_pairs={{0,32},{64,96},{128,160},{192,224},{256,288},{320,352},{384,416},{... | collective-permute-start | bytes 1769480 | tf_op jit(solution)/shard_map/ppermute | solution.py:347
  70.1 5.6 %copy-start.1 = (f32[7]{0:T(128)S(1)}, f32[7]{0:T(128)}, u32[]{:S(2)}) copy-start(f32[7]{0:T(128)} %limit_ref.1) | copy-start | bytes 88

commit v4 on v3

--- a/solution.py
+++ b/solution.py
@@ -89,24 +89,40 @@
     count = rank_positions(in_ref, source, count_ref, new_ref, own_ref, tags_vm, tags_sm, sem)
     even = lax.axis_index("node") % 2 == 0
 
-    def quantity(q, carry):
+    def gather(q, base):
+        rows = pl.ds(base, GROUP)
         for half in range(HALVES):
             lanes = slice(half * LANES, (half + 1) * LANES)
-            for p in range(NEW_CAP):
+            for p in range(GROUP):
                 for part in range(2):
                     tile = half * HALF_TILES + 2 * q + part
-                    cells = in_ref[source[p], tile].astype(jnp.float32)
+                    cells = in_ref[source[base + p], tile].astype(jnp.float32)
                     start = p * PITCH + part * 8
-                    work[half, start : start + 8, :] = jnp.where(p < count, cells, 0.0)
+                    work[half, start : start + 8, :] = jnp.where(base + p < count, cells, 0.0)
             layers = []
             for c in range(EDGE):
-                layer = work[half, pl.ds(c, NEW_CAP, stride=PITCH), :]
-                out_ref[q, c, :, lanes] = layer.astype(jnp.bfloat16)
+                layer = work[half, pl.ds(c, GROUP, stride=PITCH), :]
+                out_ref[q, c, rows, lanes] = layer.astype(jnp.bfloat16)
                 layers.append(layer)
             bottom, top = outward(layers), outward(layers[::-1])
             for m in range(SENT):
-                link_ref[SENT * q + m, :, lanes] = jnp.where(even, bottom[m], top[m])
-                chip_ref[SENT * q + m, :, lanes] = jnp.where(even, top[m], bottom[m])
+                link_ref[SENT * q + m, rows, lanes] = jnp.where(even, bottom[m], top[m])
+                chip_ref[SENT * q + m, rows, lanes] = jnp.where(even, top[m], bottom[m])
+
+    def quantity(q, carry):
+        for index in range(NEW_CAP // GROUP):
+            base = index * GROUP
+
+            @pl.when(base < count)
+            def _(base=base):
+                gather(q, base)
+
+            @pl.when(base >= count)
+            def _(base=base):
+                empty = jnp.zeros((SENT, GROUP, PLANE), jnp.bfloat16)
+                for ref in (link_ref, chip_ref):
+                    ref[pl.ds(SENT * q, SENT), base : base + GROUP, :] = empty
+
         return carry
 
     lax.fori_loop(0, QUANT, quantity, 0)
@@ -147,14 +163,14 @@
             yield k - 4, 0.75 * (cells[c] + cells[c + 1]) + (shift - 0.5 * bends[c])
 
 
-def tiles(body_of):
+def tiles(count, body_of):
     def tile(index, carry):
         half = index % HALVES
         base = pl.multiple_of((index // HALVES) * GROUP, GROUP)
         body_of(base, pl.ds(base, GROUP), pl.ds(pl.multiple_of(half * LANES, LANES), LANES))
         return carry
 
-    lax.fori_loop(0, HALVES * (NEW_CAP // GROUP), tile, 0)
+    lax.fori_loop(0, HALVES * pl.cdiv(count, GROUP), tile, 0)
 
 
 def by_direction(speed_ref, q, run):
@@ -167,7 +183,9 @@
         run(q, False)
 
 
-def inner_kernel(speed_ref, in_ref, mid_ref):
+def inner_kernel(speed_ref, count_ref, in_ref, mid_ref):
+    count = count_ref[0]
+
     def run(q, forward):
         rate = (COURANT * 2.0 / 3.0) * jnp.abs(speed_ref[q])
 
@@ -185,7 +203,7 @@
                 last = state
             mid_ref[q, EDGE - 4, rows, lanes] = last
 
-        tiles(tile)
+        tiles(count, tile)
 
     def quantity(q, carry):
         by_direction(speed_ref, q, run)
@@ -267,7 +285,7 @@
                 cells = jnp.where(base + p < count, cells, 0.0)
                 done[q, base + p, :, lanes] = cells.astype(jnp.bfloat16)
 
-        tiles(tile)
+        tiles(count, tile)
 
     def copy(q):
         return pltpu.make_async_copy(done.at[q], out_ref.at[:, q], sems.at[q])
@@ -277,6 +295,11 @@
             @pl.when((even == (speed_ref[q] >= 0.0)) == link_first)
             def _(link_first=link_first):
                 by_direction(speed_ref, q, functools.partial(run, link_first=link_first))
+
+        for base in range(0, NEW_CAP, GROUP):
+            @pl.when(base >= count)
+            def _(base=base):
+                done[q, base : base + GROUP] = jnp.zeros((GROUP, EDGE, PLANE), jnp.bfloat16)
 
         copy(q).start()
         return carry
@@ -334,7 +357,7 @@
             struct((NEW_CAP,), jnp.int32),
         ),
         scratch_shapes=[
-            pltpu.VMEM((HALVES, NEW_CAP * PITCH + 8, LANES), jnp.float32),
+            pltpu.VMEM((HALVES, GROUP * PITCH + 8, LANES), jnp.float32),
             pltpu.SMEM((NEW_CAP,), jnp.int32),
             pltpu.VMEM((owners, LANES), jnp.int32),
             pltpu.SMEM((owners, LANES), jnp.int32),
@@ -347,7 +370,7 @@
     from_chip = lax.ppermute(for_chip, "node", swaps(0, count))
     inner = pl.pallas_call(
         inner_kernel,
-        in_specs=[SMEM, VMEM],
+        in_specs=[SMEM, SMEM, VMEM],
         out_specs=VMEM,
         out_shape=pltpu.VMEM((QUANT, EDGE - 3, NEW_CAP, PLANE), jnp.float32),
         compiler_params=PARAMS,
@@ -355,7 +378,7 @@
             flops=40 * QUANT * EDGE * NEW_CAP * PLANE, transcendentals=0, bytes_accessed=0
         ),
         name="inner",
-    )(speeds, near(arranged))
+    )(speeds, total, near(arranged))
     updated = pl.pallas_call(
         outer_kernel,
         in_specs=[SMEM, SMEM, SMEM, VMEM, VMEM, VMEM, VMEM, VMEM],

time: 81.3 us -> 80.9 us (level)
  transfers between devices with their start and end apart: 2 -> 2, of which waited for: 1 -> 0; matrix products, arithmetic and copies ran while one was open for 0% -> 0% of each run, Pallas kernels for 6% -> 7%
where the time goes in v4:
time: 80.9 us; the launch traced here: 80.8 us
  blocking collectives  54.2 us (67%)
  Pallas kernels  16.2 us (20%)
  starting transfers between devices  9.62 us (12%)
    all_to_all x1, blocking collectives, body(): lax.all_to_all(outgoing, 'dev', split_axis=0, concat_axis=0, tiled=True)  54.2 us
    ppermute x1, starting transfers between devices, body(): from_link = lax.ppermute(for_link, 'node', swaps(1, count))  7.7 us
    pallas_call x1, Pallas kernels, body(): pl.pallas_call(inner_kernel, in_specs=[SMEM, SMEM, VMEM], out_specs=VMEM,...  5.72 us
    pallas_call x1, Pallas kernels, body(): pl.pallas_call(outer_kernel, in_specs=[SMEM, SMEM, SMEM, VMEM, VMEM, VMEM...  5.4 us
    pallas_call x1, Pallas kernels, body(): pl.pallas_call(arrange_kernel, in_specs=[VMEM], out_specs=(VMEM, VMEM, VM...  2.94 us
    pallas_call x1, Pallas kernels, body(): pl.pallas_call(pack_kernel, in_specs=[SMEM, SMEM, ANY], out_specs=VMEM, o...  2.12 us
    ppermute x1, starting transfers between devices, body(): from_chip = lax.ppermute(for_chip, 'node', swaps(0, count))  1.92 us
  transfers between devices with their start and end apart: 2, of which 0 were waited for; matrix products, arithmetic and copies ran while one was open for 0% of the time, Pallas kernels for 7%

profile of v4, /device:TPU:449, one launch (start us, length us, event | category | flops | bytes accessed | tf_op | source)
XLA Modules:
  0.0 80.8 jit_solution(11184792473946484628)
XLA Ops:
  0.6 2.1 %pack.1 = bf16[32,29,8,128]{3,2,1,0:T(8,128)(2,1)S(1)} custom-call(s32[1,1,16]{2,1,0:T(1,128)} %dest_ref.1, s32[1,1,16]{2,1,0:T(1,128)} %level_ref.1, bf16[16,14,8,256]{3,2,1,0:T(8,128)(2,1)} %bitcast.4), custom_call_target="tpu_custom_call" | custom-call | tf_op jit(solution)/shard_map/pack/pallas_call | solution.py:336
  2.8 54.2 %all_to_all.5.in_ref = bf16[32,29,8,128]{3,2,1,0:T(8,128)(2,1)S(1)} all-to-all(bf16[32,29,8,128]{3,2,1,0:T(8,128)(2,1)S(1)} %pack.1), channel_id=1, replica_groups=mesh['node'=32,'dev'=32] {'dev'}, dimensions={0} | all-to-all | bytes 3801088 | tf_op jit(solution)/shard_map/all_to_all | solution.py:345
  57.0 0.0 copy-start
  57.0 2.9 %arrange.1 = (bf16[7,16,32,256]{3,2,1,0:T(8,128)(2,1)S(1)}, bf16[36,32,256]{2,1,0:T(8,128)(2,1)S(1)}, bf16[36,32,256]{2,1,0:T(8,128)(2,1)S(1)}, s32[32,128]{1,0:T(8,128)S(1)}, s32[1]{0:T(128)}, /*index=5*/s32[32]{0:T(128)}) custom-call(bf16[32,29,8,128]{3,2,1,0:T(8,128)(2,1)S(1)} %all_to_all.5.in_ref), custom_call_target="tpu_custom_call" | custom-call | tf_op jit(solution)/shard_map/arrange/pallas_call | solution.py:347
  59.9 7.7 %collective-permute-start = (bf16[36,32,256]{2,1,0:T(8,128)(2,1)S(1)}, bf16[36,32,256]{2,1,0:T(8,128)(2,1)S(1)}, u32[]{:S(2)}, u32[]{:S(2)}) collective-permute-start(bf16[36,32,256]{2,1,0:T(8,128)(2,1)S(1)} %get-tuple-element.11), channel_id=1, source_target_pairs={{32,64},{96,128},{160,192},{224,256},{288,320},{352,384},{416,448}... | collective-permute-start | bytes 1769480 | tf_op jit(solution)/shard_map/ppermute | solution.py:369
  67.6 1.9 %collective-permute-start.1 = (bf16[36,32,256]{2,1,0:T(8,128)(2,1)S(1)}, bf16[36,32,256]{2,1,0:T(8,128)(2,1)S(1)}, u32[]{:S(2)}, u32[]{:S(2)}) collective-permute-start(bf16[36,32,256]{2,1,0:T(8,128)(2,1)S(1)} %get-tuple-element.12), channel_id=1, source_target_pairs={{0,32},{64,96},{128,160},{192,224},{256,288},{320,352},{384,416},{... | collective-permute-start | bytes 1769480 | tf_op jit(solution)/shard_map/ppermute | solution.py:370
  69.6 0.0 copy-done
  69.6 0.0 copy-start.1
  69.6 5.7 %inner.1.mid_ref = f32[7,13,32,256]{3,2,1,0:T(8,128)S(1)} custom-call(f32[7]{0:T(128)S(1)} %copy-done, s32[1]{0:T(128)} %get-tuple-element.8.count_ref, bf16[7,16,32,256]{3,2,1,0:T(8,128)(2,1)S(1)} %get-tuple-element.10.in_ref), custom_call_target="tpu_custom_call" | custom-call | flops 36700160 | tf_op jit(solution)/shard_map/inner/pallas_call | solution.py:371
  75.3 0.0 collective-permute-done.link_ref
  75.3 0.0 collective-permute-done.1.chip_ref
  75.3 0.0 copy-done.1
  75.4 5.4 %outer.1 = bf16[32,7,16,256]{3,2,1,0:T(8,128)(2,1)} custom-call(f32[7]{0:T(128)S(1)} %copy-done, f32[7]{0:T(128)S(1)} %copy-done.1, s32[1]{0:T(128)} %get-tuple-element.8.count_ref, s32[32,128]{1,0:T(8,128)S(1)} %get-tuple-element.9.own_ref, bf16[7,16,32,256]{3,2,1,0:T(8,128)(2,1)S(1)} %get-tuple-element.10.in_ref, f32[7,13,32,256]{3,2,1,0:T(8,128)S(1)} %inner.1.mid_ref, ...), custom_call_target="tpu_custom_call" | custom-call | tf_op jit(solution)/shard_map/outer/pallas_call | solution.py:382
Async XLA Ops:
  57.0 12.6 %copy-start = (f32[7]{0:T(128)S(1)}, f32[7]{0:T(128)}, u32[]{:S(2)}) copy-start(f32[7]{0:T(128)} %speed_ref.3) | copy-start | bytes 88
  59.9 15.4 %collective-permute-start = (bf16[36,32,256]{2,1,0:T(8,128)(2,1)S(1)}, bf16[36,32,256]{2,1,0:T(8,128)(2,1)S(1)}, u32[]{:S(2)}, u32[]{:S(2)}) collective-permute-start(bf16[36,32,256]{2,1,0:T(8,128)(2,1)S(1)} %get-tuple-element.11), channel_id=1, source_target_pairs={{32,64},{96,128},{160,192},{224,256},{288,320},{352,384},{416,448}... | collective-permute-start | bytes 1769480 | tf_op jit(solution)/shard_map/ppermute | solution.py:369
  67.6 7.7 %collective-permute-start.1 = (bf16[36,32,256]{2,1,0:T(8,128)(2,1)S(1)}, bf16[36,32,256]{2,1,0:T(8,128)(2,1)S(1)}, u32[]{:S(2)}, u32[]{:S(2)}) collective-permute-start(bf16[36,32,256]{2,1,0:T(8,128)(2,1)S(1)} %get-tuple-element.12), channel_id=1, source_target_pairs={{0,32},{64,96},{128,160},{192,224},{256,288},{320,352},{384,416},{... | collective-permute-start | bytes 1769480 | tf_op jit(solution)/shard_map/ppermute | solution.py:370
  69.6 5.8 %copy-start.1 = (f32[7]{0:T(128)S(1)}, f32[7]{0:T(128)}, u32[]{:S(2)}) copy-start(f32[7]{0:T(128)} %limit_ref.1) | copy-start | bytes 88

commit v5 on v4

--- a/solution.py
+++ b/solution.py
@@ -48,7 +48,7 @@
         copy.wait()
 
 
-def rank_positions(in_ref, source, count_ref, new_ref, own_ref, tags_vm, tags_sm, sem):
+def rank_positions(in_ref, source, new_ref, own_ref, tags_vm, tags_sm, sem):
     for i in range(NEW_CAP):
         tile = in_ref[i, ROW_TILES - 1].astype(jnp.float32)
         tags_vm[i : i + 1, :] = tile[0:1].astype(jnp.int32)
@@ -59,20 +59,19 @@
         source[p] = 0
         new_ref[p] = -1
     copy.wait()
-    count = jnp.int32(0)
+    count = 0
     for i in range(NEW_CAP):
         tag = tags_sm[i, 0]
-        here = tag > 0
-
-        @pl.when(here)
-        def _(i=i, tag=tag, count=count):
-            source[count] = i
-            new_ref[count] = tag - 1
-            own_ref[pl.ds(count, 1), :] = tags_vm[pl.ds(i, 1), :]
-
-        count = count + here.astype(jnp.int32)
-    count_ref[0] = count
+        source[count] = i
+        new_ref[count] = tag - 1
+        own_ref[pl.ds(count, 1), :] = tags_vm[i : i + 1, :]
+        count = count + (tag > 0).astype(jnp.int32)
     return count
+
+
+def occupied(own_ref):
+    held = jnp.where(own_ref[...] > 0, 1.0 / LANES, 0.0)
+    return jnp.sum(held).astype(jnp.int32)
 
 
 def outward(layers):
@@ -83,10 +82,10 @@
 
 
 def arrange_kernel(
-    in_ref, out_ref, link_ref, chip_ref, own_ref, count_ref, new_ref,
+    in_ref, out_ref, link_ref, chip_ref, own_ref, new_ref,
     work, source, tags_vm, tags_sm, sem,
 ):
-    count = rank_positions(in_ref, source, count_ref, new_ref, own_ref, tags_vm, tags_sm, sem)
+    count = rank_positions(in_ref, source, new_ref, own_ref, tags_vm, tags_sm, sem)
     even = lax.axis_index("node") % 2 == 0
 
     def gather(q, base):
@@ -183,8 +182,8 @@
         run(q, False)
 
 
-def inner_kernel(speed_ref, count_ref, in_ref, mid_ref):
-    count = count_ref[0]
+def inner_kernel(speed_ref, own_ref, in_ref, mid_ref):
+    count = occupied(own_ref)
 
     def run(q, forward):
         rate = (COURANT * 2.0 / 3.0) * jnp.abs(speed_ref[q])
@@ -213,10 +212,10 @@
 
 
 def outer_kernel(
-    speed_ref, limit_ref, count_ref, own_ref, in_ref, mid_ref, link_ref, chip_ref, out_ref,
-    done, work, sems,
+    speed_ref, limit_ref, own_ref, in_ref, mid_ref, link_ref, chip_ref, out_ref,
+    done, blank, work, sems,
 ):
-    count = count_ref[0]
+    count = occupied(own_ref)
     even = lax.axis_index("node") % 2 == 0
 
     def run(q, forward, link_first):
@@ -287,8 +286,22 @@
 
         tiles(count, tile)
 
-    def copy(q):
-        return pltpu.make_async_copy(done.at[q], out_ref.at[:, q], sems.at[q])
+    groups = range(NEW_CAP // GROUP)
+
+    def copy(q, g, held):
+        rows = pl.ds(g * GROUP, GROUP)
+        source = done.at[q, rows] if held else blank
+        return pltpu.make_async_copy(source, out_ref.at[rows, q], sems.at[q, g])
+
+    def each(q, held, act):
+        for g in groups:
+            @pl.when((g * GROUP < count) == held)
+            def _(g=g):
+                act(copy(q, g, held))
+
+    blank[...] = jnp.zeros_like(blank)
+    for q in range(QUANT):
+        each(q, False, lambda dma: dma.start())
 
     def quantity(q, carry):
         for link_first in (True, False):
@@ -296,17 +309,13 @@
             def _(link_first=link_first):
                 by_direction(speed_ref, q, functools.partial(run, link_first=link_first))
 
-        for base in range(0, NEW_CAP, GROUP):
-            @pl.when(base >= count)
-            def _(base=base):
-                done[q, base : base + GROUP] = jnp.zeros((GROUP, EDGE, PLANE), jnp.bfloat16)
-
-        copy(q).start()
+        each(q, True, lambda dma: dma.start())
         return carry
 
     lax.fori_loop(0, QUANT, quantity, 0)
     for q in range(QUANT):
-        copy(q).wait()
+        for held in (False, True):
+            each(q, held, lambda dma: dma.wait())
 
 
 PARAMS = pltpu.CompilerParams(vmem_limit_bytes=24 << 20)
@@ -344,16 +353,15 @@
     )(far(destinations), far(levels), far(blocks.reshape(SLOTS, HALF_TILES, 8, PLANE)))
     incoming = lax.all_to_all(outgoing, "dev", split_axis=0, concat_axis=0, tiled=True)
     sent = struct((SENT * QUANT + 1, NEW_CAP, PLANE), jnp.bfloat16)
-    arranged, for_link, for_chip, own, total, new_levels = pl.pallas_call(
+    arranged, for_link, for_chip, own, new_levels = pl.pallas_call(
         arrange_kernel,
         in_specs=[VMEM],
-        out_specs=(VMEM, VMEM, VMEM, VMEM, SMEM, SMEM),
+        out_specs=(VMEM, VMEM, VMEM, VMEM, SMEM),
         out_shape=(
             pltpu.VMEM((QUANT, EDGE, NEW_CAP, PLANE), jnp.bfloat16),
             sent,
             sent,
             pltpu.VMEM((NEW_CAP, LANES), jnp.int32),
-            struct((1,), jnp.int32),
             struct((NEW_CAP,), jnp.int32),
         ),
         scratch_shapes=[
@@ -370,7 +378,7 @@
     from_chip = lax.ppermute(for_chip, "node", swaps(0, count))
     inner = pl.pallas_call(
         inner_kernel,
-        in_specs=[SMEM, SMEM, VMEM],
+        in_specs=[SMEM, VMEM, VMEM],
         out_specs=VMEM,
         out_shape=pltpu.VMEM((QUANT, EDGE - 3, NEW_CAP, PLANE), jnp.float32),
         compiler_params=PARAMS,
@@ -378,21 +386,22 @@
             flops=40 * QUANT * EDGE * NEW_CAP * PLANE, transcendentals=0, bytes_accessed=0
         ),
         name="inner",
-    )(speeds, total, near(arranged))
+    )(speeds, near(own), near(arranged))
     updated = pl.pallas_call(
         outer_kernel,
-        in_specs=[SMEM, SMEM, SMEM, VMEM, VMEM, VMEM, VMEM, VMEM],
+        in_specs=[SMEM, SMEM, VMEM, VMEM, VMEM, VMEM, VMEM],
         out_specs=ANY,
         out_shape=struct((NEW_CAP, QUANT, EDGE, PLANE), jnp.bfloat16),
         scratch_shapes=[
             pltpu.VMEM((QUANT, NEW_CAP, EDGE, PLANE), jnp.bfloat16),
+            pltpu.VMEM((GROUP, EDGE, PLANE), jnp.bfloat16),
             pltpu.VMEM((GROUP * PITCH + 8, LANES), jnp.float32),
-            pltpu.SemaphoreType.DMA((QUANT,)),
+            pltpu.SemaphoreType.DMA((QUANT, NEW_CAP // GROUP)),
         ],
         compiler_params=PARAMS,
         name="outer",
     )(
-        speeds, thresholds, total, near(own), near(arranged), near(inner),
+        speeds, thresholds, near(own), near(arranged), near(inner),
         near(from_link), near(from_chip),
     )
     return (

time: 80.9 us -> 79.7 us (0.985)
  the two profiles are of different devices: /device:TPU:449 before, /device:TPU:453 now
where the time goes in v5:
time: 79.7 us; the launch traced here: 79.6 us
  blocking collectives  54.7 us (69%)
  Pallas kernels  15 us (19%)
  starting transfers between devices  8.77 us (11%)
    all_to_all x1, blocking collectives, body(): lax.all_to_all(outgoing, 'dev', split_axis=0, concat_axis=0, tiled=True)  54.7 us
    ppermute x1, starting transfers between devices, body(): from_link = lax.ppermute(for_link, 'node', swaps(1, count))  6.85 us
    pallas_call x1, Pallas kernels, body(): pl.pallas_call(inner_kernel, in_specs=[SMEM, VMEM, VMEM], out_specs=VMEM,...  5.22 us
    pallas_call x1, Pallas kernels, body(): pl.pallas_call(outer_kernel, in_specs=[SMEM, SMEM, VMEM, VMEM, VMEM, VMEM...  4.9 us
    pallas_call x1, Pallas kernels, body(): pl.pallas_call(arrange_kernel, in_specs=[VMEM], out_specs=(VMEM, VMEM, VM...  2.8 us
    pallas_call x1, Pallas kernels, body(): pl.pallas_call(pack_kernel, in_specs=[SMEM, SMEM, ANY], out_specs=VMEM, o...  2.12 us
    ppermute x1, starting transfers between devices, body(): from_chip = lax.ppermute(for_chip, 'node', swaps(0, count))  1.92 us
  transfers between devices with their start and end apart: 2, of which 1 were waited for; matrix products, arithmetic and copies ran while one was open for 0% of the time, Pallas kernels for 7%

profile of v5, /device:TPU:453, one launch (start us, length us, event | category | flops | bytes accessed | tf_op | source)
XLA Modules:
  0.0 79.6 jit_solution(4028324370161614510)
XLA Ops:
  0.6 2.1 %pack.1 = bf16[32,29,8,128]{3,2,1,0:T(8,128)(2,1)S(1)} custom-call(s32[1,1,16]{2,1,0:T(1,128)} %dest_ref.1, s32[1,1,16]{2,1,0:T(1,128)} %level_ref.1, bf16[16,14,8,256]{3,2,1,0:T(8,128)(2,1)} %bitcast.4), custom_call_target="tpu_custom_call" | custom-call | tf_op jit(solution)/shard_map/pack/pallas_call | solution.py:345
  2.8 54.7 %all_to_all.5.in_ref = bf16[32,29,8,128]{3,2,1,0:T(8,128)(2,1)S(1)} all-to-all(bf16[32,29,8,128]{3,2,1,0:T(8,128)(2,1)S(1)} %pack.1), channel_id=1, replica_groups=mesh['node'=32,'dev'=32] {'dev'}, dimensions={0} | all-to-all | bytes 3801088 | tf_op jit(solution)/shard_map/all_to_all | solution.py:354
  57.5 0.0 copy-start
  57.5 2.8 %arrange.1 = (bf16[7,16,32,256]{3,2,1,0:T(8,128)(2,1)S(1)}, bf16[36,32,256]{2,1,0:T(8,128)(2,1)S(1)}, bf16[36,32,256]{2,1,0:T(8,128)(2,1)S(1)}, s32[32,128]{1,0:T(8,128)S(1)}, s32[32]{0:T(128)}) custom-call(bf16[32,29,8,128]{3,2,1,0:T(8,128)(2,1)S(1)} %all_to_all.5.in_ref), custom_call_target="tpu_custom_call" | custom-call | tf_op jit(solution)/shard_map/arrange/pallas_call | solution.py:356
  60.3 6.9 %collective-permute-start = (bf16[36,32,256]{2,1,0:T(8,128)(2,1)S(1)}, bf16[36,32,256]{2,1,0:T(8,128)(2,1)S(1)}, u32[]{:S(2)}, u32[]{:S(2)}) collective-permute-start(bf16[36,32,256]{2,1,0:T(8,128)(2,1)S(1)} %get-tuple-element.9), channel_id=1, source_target_pairs={{32,64},{96,128},{160,192},{224,256},{288,320},{352,384},{416,448}... | collective-permute-start | bytes 1769480 | tf_op jit(solution)/shard_map/ppermute | solution.py:377
  67.2 1.9 %collective-permute-start.1 = (bf16[36,32,256]{2,1,0:T(8,128)(2,1)S(1)}, bf16[36,32,256]{2,1,0:T(8,128)(2,1)S(1)}, u32[]{:S(2)}, u32[]{:S(2)}) collective-permute-start(bf16[36,32,256]{2,1,0:T(8,128)(2,1)S(1)} %get-tuple-element.10), channel_id=1, source_target_pairs={{0,32},{64,96},{128,160},{192,224},{256,288},{320,352},{384,416},{... | collective-permute-start | bytes 1769480 | tf_op jit(solution)/shard_map/ppermute | solution.py:378
  69.1 0.0 copy-done
  69.1 0.0 copy-start.1
  69.1 5.2 %inner.1.mid_ref = f32[7,13,32,256]{3,2,1,0:T(8,128)S(1)} custom-call(f32[7]{0:T(128)S(1)} %copy-done, s32[32,128]{1,0:T(8,128)S(1)} %get-tuple-element.7.own_ref, bf16[7,16,32,256]{3,2,1,0:T(8,128)(2,1)S(1)} %get-tuple-element.8.in_ref), custom_call_target="tpu_custom_call" | custom-call | flops 36700160 | tf_op jit(solution)/shard_map/inner/pallas_call | solution.py:379
  74.3 0.4 collective-permute-done.link_ref
  74.7 0.0 collective-permute-done.1.chip_ref
  74.7 0.0 copy-done.1
  74.7 4.9 %outer.1 = bf16[32,7,16,256]{3,2,1,0:T(8,128)(2,1)} custom-call(f32[7]{0:T(128)S(1)} %copy-done, f32[7]{0:T(128)S(1)} %copy-done.1, s32[32,128]{1,0:T(8,128)S(1)} %get-tuple-element.7.own_ref, bf16[7,16,32,256]{3,2,1,0:T(8,128)(2,1)S(1)} %get-tuple-element.8.in_ref, f32[7,13,32,256]{3,2,1,0:T(8,128)S(1)} %inner.1.mid_ref, ...), custom_call_target="tpu_custom_call" | custom-call | tf_op jit(solution)/shard_map/outer/pallas_call | solution.py:390
Async XLA Ops:
  57.5 11.6 %copy-start = (f32[7]{0:T(128)S(1)}, f32[7]{0:T(128)}, u32[]{:S(2)}) copy-start(f32[7]{0:T(128)} %speed_ref.3) | copy-start | bytes 88
  60.3 14.4 %collective-permute-start = (bf16[36,32,256]{2,1,0:T(8,128)(2,1)S(1)}, bf16[36,32,256]{2,1,0:T(8,128)(2,1)S(1)}, u32[]{:S(2)}, u32[]{:S(2)}) collective-permute-start(bf16[36,32,256]{2,1,0:T(8,128)(2,1)S(1)} %get-tuple-element.9), channel_id=1, source_target_pairs={{32,64},{96,128},{160,192},{224,256},{288,320},{352,384},{416,448}... | collective-permute-start | bytes 1769480 | tf_op jit(solution)/shard_map/ppermute | solution.py:377
  67.2 7.6 %collective-permute-start.1 = (bf16[36,32,256]{2,1,0:T(8,128)(2,1)S(1)}, bf16[36,32,256]{2,1,0:T(8,128)(2,1)S(1)}, u32[]{:S(2)}, u32[]{:S(2)}) collective-permute-start(bf16[36,32,256]{2,1,0:T(8,128)(2,1)S(1)} %get-tuple-element.10), channel_id=1, source_target_pairs={{0,32},{64,96},{128,160},{192,224},{256,288},{320,352},{384,416},{... | collective-permute-start | bytes 1769480 | tf_op jit(solution)/shard_map/ppermute | solution.py:378
  69.1 5.6 %copy-start.1 = (f32[7]{0:T(128)S(1)}, f32[7]{0:T(128)}, u32[]{:S(2)}) copy-start(f32[7]{0:T(128)} %limit_ref.1) | copy-start | bytes 88

commit v6 on v5

--- a/solution.py
+++ b/solution.py
@@ -19,6 +19,7 @@
 HALF_TILES = QUANT * EDGE // 8
 ROW_TILES = HALVES * HALF_TILES + 1
 SENT = 5
+LIMITS = 8
 
 COURANT = 0.4
 WENO_EPS = 1e-06
@@ -28,7 +29,9 @@
 ANY = pl.BlockSpec(memory_space=pl.ANY)
 
 
-def pack_kernel(dest_ref, level_ref, blocks_ref, out_ref, sems):
+def pack_kernel(
+    dest_ref, level_ref, speed_ref, limit_ref, blocks_ref, out_ref, params_ref, sems
+):
     last = ROW_TILES - 1
     out_ref[:, last] = jnp.zeros((out_ref.shape[0], 8, LANES), jnp.bfloat16)
     for s in range(SLOTS):
@@ -44,6 +47,10 @@
             )
             copy.start()
             copies.append(copy)
+    params_ref[...] = jnp.zeros_like(params_ref)
+    for q in range(QUANT):
+        params_ref[q : q + 1, :] = jnp.full((1, LANES), speed_ref[q])
+        params_ref[LIMITS + q : LIMITS + q + 1, :] = jnp.full((1, LANES), limit_ref[q])
     for copy in copies:
         copy.wait()
 
@@ -172,21 +179,33 @@
     lax.fori_loop(0, HALVES * pl.cdiv(count, GROUP), tile, 0)
 
 
-def by_direction(speed_ref, q, run):
-    @pl.when(speed_ref[q] >= 0.0)
+def backwards(params_ref):
+    speeds = params_ref[0:LIMITS, :]
+    row = lax.broadcasted_iota(jnp.int32, speeds.shape, 0)
+    bit = jnp.left_shift(1, row).astype(jnp.float32) * (1.0 / LANES)
+    return jnp.sum(jnp.where(speeds < 0.0, bit, 0.0)).astype(jnp.int32)
+
+
+def by_direction(backward, q, run):
+    @pl.when(jnp.logical_not(backward))
     def _():
         run(q, True)
 
-    @pl.when(speed_ref[q] < 0.0)
+    @pl.when(backward)
     def _():
         run(q, False)
 
 
-def inner_kernel(speed_ref, own_ref, in_ref, mid_ref):
+def moves_back(bits, q):
+    return (jnp.right_shift(bits, q) & 1) == 1
+
+
+def inner_kernel(params_ref, own_ref, in_ref, mid_ref):
     count = occupied(own_ref)
+    bits = backwards(params_ref)
 
     def run(q, forward):
-        rate = (COURANT * 2.0 / 3.0) * jnp.abs(speed_ref[q])
+        rate = (COURANT * 2.0 / 3.0) * jnp.abs(params_ref[pl.ds(q, 1), :])
 
         def tile(base, rows, lanes):
             def read(k):
@@ -205,22 +224,23 @@
         tiles(count, tile)
 
     def quantity(q, carry):
-        by_direction(speed_ref, q, run)
+        by_direction(moves_back(bits, q), q, run)
         return carry
 
     lax.fori_loop(0, QUANT, quantity, 0)
 
 
 def outer_kernel(
-    speed_ref, limit_ref, own_ref, in_ref, mid_ref, link_ref, chip_ref, out_ref,
+    params_ref, own_ref, in_ref, mid_ref, link_ref, chip_ref, out_ref,
     done, blank, work, sems,
 ):
     count = occupied(own_ref)
+    bits = backwards(params_ref)
     even = lax.axis_index("node") % 2 == 0
 
     def run(q, forward, link_first):
-        limit = limit_ref[q]
-        rate = (COURANT * 2.0 / 3.0) * jnp.abs(speed_ref[q])
+        limit = params_ref[pl.ds(LIMITS + q, 1), :]
+        rate = (COURANT * 2.0 / 3.0) * jnp.abs(params_ref[pl.ds(q, 1), :])
 
         def tile(base, rows, lanes):
             own = own_ref[rows, :].astype(jnp.float32)
@@ -304,10 +324,11 @@
         each(q, False, lambda dma: dma.start())
 
     def quantity(q, carry):
+        backward = moves_back(bits, q)
         for link_first in (True, False):
-            @pl.when((even == (speed_ref[q] >= 0.0)) == link_first)
+            @pl.when((even != backward) == link_first)
             def _(link_first=link_first):
-                by_direction(speed_ref, q, functools.partial(run, link_first=link_first))
+                by_direction(backward, q, functools.partial(run, link_first=link_first))
 
         each(q, True, lambda dma: dma.start())
         return carry
@@ -342,15 +363,21 @@
     owners = lax.axis_size("dev")
     count = lax.axis_size("node")
     row = (owners, ROW_TILES, 8, LANES)
-    outgoing = pl.pallas_call(
+    outgoing, params = pl.pallas_call(
         pack_kernel,
-        in_specs=[SMEM, SMEM, ANY],
-        out_specs=VMEM,
-        out_shape=pltpu.VMEM(row, jnp.bfloat16),
+        in_specs=[SMEM, SMEM, SMEM, SMEM, ANY],
+        out_specs=(VMEM, VMEM),
+        out_shape=(
+            pltpu.VMEM(row, jnp.bfloat16),
+            pltpu.VMEM((2 * LIMITS, LANES), jnp.float32),
+        ),
         scratch_shapes=[pltpu.SemaphoreType.DMA((SLOTS, HALVES))],
         compiler_params=PARAMS,
         name="pack",
-    )(far(destinations), far(levels), far(blocks.reshape(SLOTS, HALF_TILES, 8, PLANE)))
+    )(
+        far(destinations), far(levels), far(speeds), far(thresholds),
+        far(blocks.reshape(SLOTS, HALF_TILES, 8, PLANE)),
+    )
     incoming = lax.all_to_all(outgoing, "dev", split_axis=0, concat_axis=0, tiled=True)
     sent = struct((SENT * QUANT + 1, NEW_CAP, PLANE), jnp.bfloat16)
     arranged, for_link, for_chip, own, new_levels = pl.pallas_call(
@@ -378,7 +405,7 @@
     from_chip = lax.ppermute(for_chip, "node", swaps(0, count))
     inner = pl.pallas_call(
         inner_kernel,
-        in_specs=[SMEM, VMEM, VMEM],
+        in_specs=[VMEM, VMEM, VMEM],
         out_specs=VMEM,
         out_shape=pltpu.VMEM((QUANT, EDGE - 3, NEW_CAP, PLANE), jnp.float32),
         compiler_params=PARAMS,
@@ -386,10 +413,10 @@
             flops=40 * QUANT * EDGE * NEW_CAP * PLANE, transcendentals=0, bytes_accessed=0
         ),
         name="inner",
-    )(speeds, near(own), near(arranged))
+    )(near(params), near(own), near(arranged))
     updated = pl.pallas_call(
         outer_kernel,
-        in_specs=[SMEM, SMEM, VMEM, VMEM, VMEM, VMEM, VMEM],
+        in_specs=[VMEM, VMEM, VMEM, VMEM, VMEM, VMEM],
         out_specs=ANY,
         out_shape=struct((NEW_CAP, QUANT, EDGE, PLANE), jnp.bfloat16),
         scratch_shapes=[
@@ -401,7 +428,7 @@
         compiler_params=PARAMS,
         name="outer",
     )(
-        speeds, thresholds, near(own), near(arranged), near(inner),
+        near(params), near(own), near(arranged), near(inner),
         near(from_link), near(from_chip),
     )
     return (

time: 79.7 us -> 78.9 us (0.990)
  the two profiles are of different devices: /device:TPU:453 before, /device:TPU:449 now
where the time goes in v6:
time: 78.9 us; the launch traced here: 77.7 us
  blocking collectives  54.2 us (69%)
  starting transfers between devices  10.2 us (13%)
  Pallas kernels  9.53 us (12%)
  waiting for transfers between devices  3.16 us (4%)
    all_to_all x1, blocking collectives, body(): lax.all_to_all(outgoing, 'dev', split_axis=0, concat_axis=0, tiled=True)  54.2 us
    ppermute x1, starting transfers between devices, body(): from_link = lax.ppermute(for_link, 'node', swaps(1, count))  8.23 us
    ppermute x1, waiting for transfers between devices, body(): from_link = lax.ppermute(for_link, 'node', swaps(1, count))  3.16 us
    pallas_call x1, Pallas kernels, body(): pl.pallas_call(outer_kernel, in_specs=[VMEM, VMEM, VMEM, VMEM, VMEM, VMEM...  2.68 us
    pallas_call x1, Pallas kernels, body(): pl.pallas_call(inner_kernel, in_specs=[VMEM, VMEM, VMEM], out_specs=VMEM,...  2.46 us
    pallas_call x1, Pallas kernels, body(): pl.pallas_call(arrange_kernel, in_specs=[VMEM], out_specs=(VMEM, VMEM, VM...  2.25 us
    pallas_call x1, Pallas kernels, body(): pl.pallas_call(pack_kernel, in_specs=[SMEM, SMEM, SMEM, SMEM, ANY], out_s...  2.14 us
    ppermute x1, starting transfers between devices, body(): from_chip = lax.ppermute(for_chip, 'node', swaps(0, count))  1.92 us
  transfers between devices with their start and end apart: 2, of which 1 were waited for; matrix products, arithmetic and copies ran while one was open for 0% of the time, Pallas kernels for 3%

profile of v6, /device:TPU:449, one launch (start us, length us, event | category | flops | bytes accessed | tf_op | source)
XLA Modules:
  0.0 77.7 jit_solution(13891047225585139192)
XLA Ops:
  0.6 2.1 %pack.1 = (bf16[32,29,8,128]{3,2,1,0:T(8,128)(2,1)S(1)}, f32[16,128]{1,0:T(8,128)S(1)}) custom-call(s32[1,1,16]{2,1,0:T(1,128)} %dest_ref.1, s32[1,1,16]{2,1,0:T(1,128)} %level_ref.1, f32[7]{0:T(128)} %speed_ref.1, f32[7]{0:T(128)} %limit_ref.1, bf16[16,14,8,256]{3,2,1,0:T(8,128)(2,1)} %bitcast.4), custom_call_target="tpu_custom_call" | custom-call | tf_op jit(solution)/shard_map/pack/pallas_call | solution.py:366
  2.8 54.2 %all_to_all.5.in_ref = bf16[32,29,8,128]{3,2,1,0:T(8,128)(2,1)S(1)} all-to-all(bf16[32,29,8,128]{3,2,1,0:T(8,128)(2,1)S(1)} %get-tuple-element.10), channel_id=1, replica_groups=mesh['node'=32,'dev'=32] {'dev'}, dimensions={0} | all-to-all | bytes 3801088 | tf_op jit(solution)/shard_map/all_to_all | solution.py:381
  57.0 2.3 %arrange.1 = (bf16[7,16,32,256]{3,2,1,0:T(8,128)(2,1)S(1)}, bf16[36,32,256]{2,1,0:T(8,128)(2,1)S(1)}, bf16[36,32,256]{2,1,0:T(8,128)(2,1)S(1)}, s32[32,128]{1,0:T(8,128)S(1)}, s32[32]{0:T(128)}) custom-call(bf16[32,29,8,128]{3,2,1,0:T(8,128)(2,1)S(1)} %all_to_all.5.in_ref), custom_call_target="tpu_custom_call" | custom-call | tf_op jit(solution)/shard_map/arrange/pallas_call | solution.py:383
  59.3 8.2 %collective-permute-start = (bf16[36,32,256]{2,1,0:T(8,128)(2,1)S(1)}, bf16[36,32,256]{2,1,0:T(8,128)(2,1)S(1)}, u32[]{:S(2)}, u32[]{:S(2)}) collective-permute-start(bf16[36,32,256]{2,1,0:T(8,128)(2,1)S(1)} %get-tuple-element.13), channel_id=1, source_target_pairs={{32,64},{96,128},{160,192},{224,256},{288,320},{352,384},{416,448}... | collective-permute-start | bytes 1769480 | tf_op jit(solution)/shard_map/ppermute | solution.py:404
  67.5 1.9 %collective-permute-start.1 = (bf16[36,32,256]{2,1,0:T(8,128)(2,1)S(1)}, bf16[36,32,256]{2,1,0:T(8,128)(2,1)S(1)}, u32[]{:S(2)}, u32[]{:S(2)}) collective-permute-start(bf16[36,32,256]{2,1,0:T(8,128)(2,1)S(1)} %get-tuple-element.14), channel_id=1, source_target_pairs={{0,32},{64,96},{128,160},{192,224},{256,288},{320,352},{384,416},{... | collective-permute-start | bytes 1769480 | tf_op jit(solution)/shard_map/ppermute | solution.py:405
  69.4 2.5 %inner.1.mid_ref = f32[7,13,32,256]{3,2,1,0:T(8,128)S(1)} custom-call(f32[16,128]{1,0:T(8,128)S(1)} %get-tuple-element.9.params_ref, s32[32,128]{1,0:T(8,128)S(1)} %get-tuple-element.11.own_ref, bf16[7,16,32,256]{3,2,1,0:T(8,128)(2,1)S(1)} %get-tuple-element.12.in_ref), custom_call_target="tpu_custom_call" | custom-call | flops 36700160 | tf_op jit(solution)/shard_map/inner/pallas_call | solution.py:406
  71.9 3.2 %collective-permute-done.link_ref = bf16[36,32,256]{2,1,0:T(8,128)(2,1)S(1)} collective-permute-done((bf16[36,32,256]{2,1,0:T(8,128)(2,1)S(1)}, bf16[36,32,256]{2,1,0:T(8,128)(2,1)S(1)}, u32[]{:S(2)}, u32[]{:S(2)}) %collective-permute-start) | collective-permute-done | bytes 589856 | tf_op jit(solution)/shard_map/ppermute | solution.py:404
  75.1 0.0 collective-permute-done.1.chip_ref
  75.1 2.7 %outer.1 = bf16[32,7,16,256]{3,2,1,0:T(8,128)(2,1)} custom-call(f32[16,128]{1,0:T(8,128)S(1)} %get-tuple-element.9.params_ref, s32[32,128]{1,0:T(8,128)S(1)} %get-tuple-element.11.own_ref, bf16[7,16,32,256]{3,2,1,0:T(8,128)(2,1)S(1)} %get-tuple-element.12.in_ref, f32[7,13,32,256]{3,2,1,0:T(8,128)S(1)} %inner.1.mid_ref, ...), custom_call_target="tpu_custom_call" | custom-call | tf_op jit(solution)/shard_map/outer/pallas_call | solution.py:417
Async XLA Ops:
  59.3 15.8 %collective-permute-start = (bf16[36,32,256]{2,1,0:T(8,128)(2,1)S(1)}, bf16[36,32,256]{2,1,0:T(8,128)(2,1)S(1)}, u32[]{:S(2)}, u32[]{:S(2)}) collective-permute-start(bf16[36,32,256]{2,1,0:T(8,128)(2,1)S(1)} %get-tuple-element.13), channel_id=1, source_target_pairs={{32,64},{96,128},{160,192},{224,256},{288,320},{352,384},{416,448}... | collective-permute-start | bytes 1769480 | tf_op jit(solution)/shard_map/ppermute | solution.py:404
  67.5 7.6 %collective-permute-start.1 = (bf16[36,32,256]{2,1,0:T(8,128)(2,1)S(1)}, bf16[36,32,256]{2,1,0:T(8,128)(2,1)S(1)}, u32[]{:S(2)}, u32[]{:S(2)}) collective-permute-start(bf16[36,32,256]{2,1,0:T(8,128)(2,1)S(1)} %get-tuple-element.14), channel_id=1, source_target_pairs={{0,32},{64,96},{128,160},{192,224},{256,288},{320,352},{384,416},{... | collective-permute-start | bytes 1769480 | tf_op jit(solution)/shard_map/ppermute | solution.py:405
